TPU v7x, 16 devices: a whole 2x2x2 slice. The times are simulated.
16 devices in a mesh: rep: 1, dp: 16 (over x, y, z, core).
Axes of the slice: x: 2, y: 2, z: 2, core: 2. Of those that a mesh axis runs over, the one named last changes fastest.
Arguments:
- x: bfloat16 [16, 2048, 512], P(('rep', 'dp'))
- dy: bfloat16 [16, 2048, 512], P(('rep', 'dp'))
- w_gate: bfloat16 [2, 512, 8192], replicated
- w_up: bfloat16 [2, 512, 8192], replicated
- w_down: bfloat16 [2, 8192, 512], replicated
- m_w_gate: float32 [2, 512, 8192], P(None, 'dp')
- m_w_up: float32 [2, 512, 8192], P(None, 'dp')
- m_w_down: float32 [2, 8192, 512], P(None, 'dp')
- v_w_gate: float32 [2, 512, 8192], P(None, 'dp')
- v_w_up: float32 [2, 512, 8192], P(None, 'dp')
- v_w_down: float32 [2, 8192, 512], P(None, 'dp')
Outputs:
- output 1: bfloat16 [2, 512, 8192], P('rep')
- output 2: bfloat16 [2, 512, 8192], P('rep')
- output 3: bfloat16 [2, 8192, 512], P('rep')
- output 4: float32 [2, 512, 8192], P('rep', 'dp')
- output 5: float32 [2, 512, 8192], P('rep', 'dp')
- output 6: float32 [2, 8192, 512], P('rep', 'dp')
- output 7: float32 [2, 512, 8192], P('rep', 'dp')
- output 8: float32 [2, 512, 8192], P('rep', 'dp')
- output 9: float32 [2, 8192, 512], P('rep', 'dp')
All inputs are finite; a program needn't handle non-finite values.
Results may differ from a plain program's by a relative error of at most 0.022.
Values are sent between devices in bfloat16 or wider.
A program may use at most 2 GiB of HBM per device.

v0:
```python
import jax
import jax.numpy as jnp
from jax import lax

NAMES = ("w_gate", "w_up", "w_down")


def matmul(a, w):
    return jnp.dot(a, w, preferred_element_type=jnp.float32).astype(jnp.bfloat16)


def normed(h):
    wide = h.astype(jnp.float32)
    scale = lax.rsqrt(jnp.mean(wide**2, -1, keepdims=True) + 1e-6)
    return (wide * scale).astype(jnp.bfloat16)


def layer(h, w):
    a = normed(h)
    gate = jnp.dot(a, w["w_gate"], preferred_element_type=jnp.float32)
    up = jnp.dot(a, w["w_up"], preferred_element_type=jnp.float32)
    return h + matmul((jax.nn.silu(gate) * up).astype(jnp.bfloat16), w["w_down"])


def adamw(w, m, v, g):
    m = 0.9 * m + 0.1 * g
    v = 0.95 * v + 0.05 * g * g
    step = m * lax.rsqrt(v + 1e-8) + 0.1 * w
    return (w - 0.02 * step).astype(jnp.bfloat16), m, v


def clipped(gradients, sum_of_squares, count):
    factor = jnp.minimum(1.0, 0.5 * lax.rsqrt(sum_of_squares / count + 1e-30))
    return [g * factor for g in gradients]


def stack(weights, h):
    for number in range(weights["w_gate"].shape[0]):
        h = layer(h, {name: w[number] for name, w in weights.items()})
    return h


def solution(mesh):
    groups = mesh.shape["rep"]

    def step(x, dy, *arrays):
        weights, m, v = (arrays[i : i + 3] for i in (0, 3, 6))
        x, dy = (t.reshape(groups, -1, *t.shape[1:]) for t in (x, dy))

        def of_a_group(x, dy):
            _, back = jax.vjp(lambda w: stack(w, x), dict(zip(NAMES, weights, strict=True)))
            by_weights = back(dy)[0]
            gradients = [by_weights[name].astype(jnp.float32) for name in NAMES]
            gradients = clipped(gradients, sum(jnp.sum(g * g) for g in gradients), sum(g.size for g in gradients))
            new = [adamw(w.astype(jnp.float32), m, v, g) for w, m, v, g in zip(weights, m, v, gradients, strict=True)]
            return tuple(one[which] for which in range(3) for one in new)

        return tuple(t.reshape(-1, *t.shape[2:]) for t in jax.vmap(of_a_group)(x, dy))

    return step
```

profile of v0, /device:TPU:0, one launch (start us, length us, event | category | flops | bytes accessed | tf_op | source)
XLA Modules:
  0.0 2358.0 jit_solution(6119364788853281992)
XLA Ops:
  13.6 29.9 %fusion.170 = f32[2048,8192]{1,0:T(8,128)} fusion(bf16[2,512,8192]{2,1,0:T(8,128)(2,1)} %param.12, bf16[1,2048,512]{1,2,0:T(8,128)(2,1)S(1)} %fusion.183), kind=kOutput, calls=%fused_computation.210 | convolution fusion | flops 17179869184 | bytes 77594624 | tf_op jit(solution)/vmap(jvp())/dot_general | solution.py:20
  43.5 62.9 %fusion.154 = (bf16[1,2048,8192]{2,1,0:T(8,128)(2,1)}, f32[2048,8192]{1,0:T(8,128)}) fusion(f32[2048,8192]{1,0:T(8,128)} %fusion.170, bf16[2,512,8192]{2,1,0:T(8,128)(2,1)} %param.17, bf16[1,2048,512]{1,2,0:T(8,128)(2,1)S(1)} %fusion.183), kind=kOutput, calls=%fused_computation.189 | convolution fusion | flops 17280532480 | bytes 178257920 | tf_op jit(solution)/vmap(jvp())/dot_general | solution.py:21
  106.3 25.6 %fusion.186 = (f32[2048]{0:T(1024)S(1)}, bf16[1,2048,512]{1,2,0:T(8,128)(2,1)}) fusion(bf16[1,2048,512]{1,2,0:T(8,128)(2,1)} %copy-done.17, bf16[2,8192,512]{2,1,0:T(8,128)(2,1)} %param.15, bf16[1,2048,8192]{2,1,0:T(8,128)(2,1)} %get-tuple-element.263), kind=kOutput, calls=%fused_computation.233 | convolution fusion | flops 17185110016 | bytes 46145536 | tf_op jit(solution)/vmap(jvp())/dot_general | solution.py:9
  134.6 29.9 %fusion.163 = f32[2048,8192]{1,0:T(8,128)} fusion(bf16[2,512,8192]{2,1,0:T(8,128)(2,1)} %param.17, bf16[1,2048,512]{1,2,0:T(8,128)(2,1)S(1)} %fusion.187), kind=kOutput, calls=%fused_computation.203 | convolution fusion | flops 17179869184 | bytes 77594624 | tf_op jit(solution)/vmap(jvp())/dot_general | solution.py:21
  164.5 25.2 %convolution_convert_fusion.1 = bf16[2048,8192]{1,0:T(8,128)(2,1)} fusion(bf16[2,8192,512]{2,1,0:T(8,128)(2,1)} %param.15, bf16[1,2048,512]{2,1,0:T(8,128)(2,1)} %param.14), kind=kOutput, calls=%fused_computation.199 | convolution fusion | flops 17196646400 | bytes 44040192 | tf_op jit(solution)/vmap(transpose(jvp()))/dot_general | solution.py:9
  189.7 87.6 %fusion.143 = (bf16[1,2048,8192]{2,1,0:T(8,128)(2,1)}, bf16[1,2048,8192]{2,1,0:T(8,128)(2,1)}, f32[2048,8192]{1,0:T(8,128)}) fusion(f32[2048,8192]{1,0:T(8,128)} %fusion.163, bf16[2048,8192]{1,0:T(8,128)(2,1)} %convolution_convert_fusion.1, bf16[2,512,8192]{2,1,0:T(8,128)(2,1)} %param.12, bf16[1,2048,512]{1,2,0:T(8,128)(2,1)S(1)} %fusion.187), kind=kOutput, calls=%fused_computation.173 | convolution fusion | flops 17431527424 | bytes 245366784 | tf_op jit(solution)/vmap(jvp())/dot_general | solution.py:20
  277.3 52.5 %fusion.153 = bf16[1,2048,8192]{2,1,0:T(8,128)(2,1)} fusion(f32[2048,8192]{1,0:T(8,128)} %fusion.163, f32[2048,8192]{1,0:T(8,128)} %get-tuple-element.267), kind=kLoop, calls=%fused_computation.187 | loop fusion | flops 100663296 | bytes 167772160 | tf_op jit(solution)/vmap(jvp())/convert_element_type | solution.py:22
  329.9 41.8 %copy.3 = bf16[1,2048,8192]{1,2,0:T(8,128)(2,1)} copy(bf16[1,2048,8192]{2,1,0:T(8,128)(2,1)} %fusion.153) | data formatting | bytes 67108864
  371.7 231.6 %while.16 = (bf16[1,2048,8192]{1,2,0:T(8,128)(2,1)}, bf16[1,2048,512]{2,1,0:T(8,128)(2,1)S(1)}, f32[512,512]{1,0:T(8,128)S(1)}, f32[512,512]{1,0:T(8,128)}, u32[...) while((bf16[1,2048,8192]{1,2,0:T(8,128)(2,1)}, ...), condition=%wide.windowed_dot_general_cond_rs.4.clone, body=%wide.windowed_dot_general_body_rs.4.clone.sunk | while | flops 4313317376 | bytes 109052488 | solution.py:9
  394.0 21.4 collective-permute-start.18
  617.7 41.6 %copy.5 = bf16[1,2048,8192]{1,2,0:T(8,128)(2,1)} copy(bf16[1,2048,8192]{2,1,0:T(8,128)(2,1)} %get-tuple-element.263) | data formatting | bytes 67108864
  659.4 24.1 %fusion.194 = bf16[2048,512]{0,1:T(8,128)(2,1)S(1)} fusion(bf16[2,512,8192]{2,1,0:T(8,128)(2,1)} %param.17, bf16[1,2048,8192]{2,1,0:T(8,128)(2,1)} %get-tuple-element.612), kind=kOutput, calls=%fused_computation.240 | convolution fusion | flops 17179869184 | bytes 44040192 | tf_op jit(solution)/vmap(transpose(jvp()))/dot_general | solution.py:21
  683.5 25.6 %fusion.188 = (f32[2048]{0:T(1024)S(1)}, bf16[1,2048,512]{1,2,0:T(8,128)(2,1)}) fusion(bf16[1,2048,512]{1,2,0:T(8,128)(2,1)S(1)} %copy-done.20, bf16[2048,512]{0,1:T(8,128)(2,1)S(1)} %fusion.194, bf16[2,512,8192]{2,1,0:T(8,128)(2,1)} %param.12, bf16[1,2048,8192]{2,1,0:T(8,128)(2,1)} %get-tuple-element.540), kind=kOutput, calls=%fused_computation.235 | convolution fusion | flops 17185110016 | bytes 48242688 | tf_op jit(solution)/vmap(transpose(jvp()))/dot_general | solution.py:20
  714.6 229.4 %while.17 = (bf16[1,2048,512]{2,1,0:T(8,128)(2,1)}, bf16[1,2048,8192]{1,2,0:T(8,128)(2,1)}, f32[512,512]{0,1:T(8,128)S(1)}, f32[512,512]{0,1:T(8,128)}, u32[]{:T...) while((bf16[1,2048,512]{2,1,0:T(8,128)(2,1)}, ...), condition=%wide.windowed_dot_general_cond_rs.5.clone, body=%wide.windowed_dot_general_body_rs.5.clone.sunk | while | flops 4313317376 | bytes 109052488 | solution.py:9
  735.6 21.4 collective-permute-start.22
  956.1 237.4 %while.14 = (bf16[1,2048,8192]{2,1,0:T(8,128)(2,1)}, bf16[1,2048,512]{1,2,0:T(8,128)(2,1)S(1)}, f32[8192,32]{0,1:T(8,128)}, f32[8192,32]{0,1:T(8,128)}, u32[]{:T...) while((bf16[1,2048,8192]{2,1,0:T(8,128)(2,1)}, ...), condition=%wide.windowed_dot_general_cond_rs.2.clone, body=%wide.windowed_dot_general_body_rs.2.clone.sunk | while | flops 4297588736 | bytes 109052488 | solution.py:21
  961.0 14.9 fusion.338
  979.2 19.7 collective-permute-start.10
  999.0 14.9 fusion.340
  1029.3 14.9 fusion.338
  1056.4 14.9 fusion.340
  1087.9 14.9 fusion.338
  1115.4 14.9 fusion.340
  1147.4 14.9 fusion.338
  1174.9 14.9 fusion.340
  1202.7 77.6 %convert_multiply_fusion = (bf16[1,2048,8192]{2,1,0:T(8,128)(2,1)}, bf16[1,2048,8192]{2,1,0:T(8,128)(2,1)}) fusion(f32[2048,8192]{1,0:T(8,128)} %fusion.170, f32[2048,8192]{1,0:T(8,128)} %get-tuple-element.264, bf16[2,8192,512]{2,1,0:T(8,128)(2,1)} %param.15, bf16[1,2048,512]{1,2,0:T(8,128)(2,1)} %copy-done.19), kind=kOutput, calls=%fused_computation.168 | convolution fusion | flops 17448304640 | bytes 211812352 | tf_op jit(solution)/vmap(transpose(jvp()))/dot_general | solution.py:9
  1280.4 235.1 %while.15 = (bf16[1,2048,8192]{2,1,0:T(8,128)(2,1)}, bf16[1,2048,512]{1,2,0:T(8,128)(2,1)S(1)}, f32[8192,32]{0,1:T(8,128)S(1)}, f32[8192,32]{0,1:T(8,128)}, u32[...) while((bf16[1,2048,8192]{2,1,0:T(8,128)(2,1)}, ...), condition=%wide.windowed_dot_general_cond_rs.3.clone, body=%wide.windowed_dot_general_body_rs.3.clone.sunk | while | flops 4297588736 | bytes 113246824 | solution.py:21
  1433.9 14.9 fusion.348
  1496.2 14.9 fusion.348
  1516.4 238.1 %while.12 = (bf16[1,2048,8192]{2,1,0:T(8,128)(2,1)}, bf16[1,2048,512]{1,2,0:T(8,128)(2,1)}, f32[8192,32]{0,1:T(8,128)}, f32[8192,32]{0,1:T(8,128)}, u32[]{:T(128...) while((bf16[1,2048,8192]{2,1,0:T(8,128)(2,1)}, ...), condition=%wide.windowed_dot_general_cond_rs.clone, body=%wide.windowed_dot_general_body_rs.clone.sunk | while | flops 4297588736 | bytes 117441128 | solution.py:20
  1532.9 17.9 fusion.322
  1558.8 14.9 fusion.324
  1590.0 17.9 fusion.322
  1616.9 14.9 fusion.324
  1650.6 17.9 fusion.322
  1677.5 14.9 fusion.324
  1709.0 17.9 fusion.322
  1735.9 14.9 fusion.324
  1754.5 237.9 %while.13 = (bf16[1,2048,8192]{2,1,0:T(8,128)(2,1)}, bf16[1,2048,512]{1,2,0:T(8,128)(2,1)S(1)}, f32[8192,32]{0,1:T(8,128)S(1)}, f32[8192,32]{0,1:T(8,128)}, u32[...) while((bf16[1,2048,8192]{2,1,0:T(8,128)(2,1)}, ...), condition=%wide.windowed_dot_general_cond_rs.1.clone, body=%wide.windowed_dot_general_body_rs.1.clone.sunk | while | flops 4297588736 | bytes 113246824 | solution.py:20
  1794.1 14.9 fusion.332
  1853.9 14.9 fusion.332
  1913.4 14.9 fusion.332
  1973.2 14.9 fusion.332
  2034.9 40.6 %all-reduce.10 = f32[]{:T(128)} all-reduce(f32[]{:T(128)S(6)} %add.180), channel_id=13, replica_groups=mesh['rep'=1,'dp'=16] {'dp'}, use_global_device_ids=true, to_apply=%region_3.4.clone | all-reduce | flops 1 | bytes 8 | tf_op jit(solution)/vmap()/reduce_sum | solution.py:54
  2094.8 64.7 %all-gather.14.cloned.1.call-done = bf16[1,2,8192,512]{3,2,1,0:T(8,128)(2,1)} async-done(((bf16[1,2,512,512]{3,2,1,0:T(8,128)(2,1)}), bf16[1,2,8192,512]{3,2,1,0:T(8,128)(2,1)}) %all-gather.14.cloned.1.call-update) | async-done | bytes 16777232 | tf_op jit(solution)/reshape | solution.py:58
  2159.5 78.9 %all-gather.12.cloned.1.call-done = bf16[1,2,512,8192]{3,2,1,0:T(8,128)(2,1)} async-done(((bf16[1,2,32,8192]{3,2,1,0:T(8,128)(2,1)}), bf16[1,2,512,8192]{3,2,1,0:T(8,128)(2,1)}) %all-gather.12.cloned.1.call-update) | async-done | bytes 16777232 | tf_op jit(solution)/reshape | solution.py:58
  2238.4 78.9 %all-gather.10.cloned.1.call-done = bf16[1,2,512,8192]{3,2,1,0:T(8,128)(2,1)} async-done(((bf16[1,2,32,8192]{3,2,1,0:T(8,128)(2,1)}), bf16[1,2,512,8192]{3,2,1,0:T(8,128)(2,1)}) %all-gather.10.cloned.1.call-update) | async-done | bytes 16777232 | tf_op jit(solution)/reshape | solution.py:58
  2317.3 16.7 copy.63
  (455 shorter events, 1133.1 us)
Async XLA Ops:
  7.2 2152.3 %all-gather.14.cloned.1.call-start = ((), (), s32[]{:S(2)}) async-start(), calls=%async_computation.2 | async-start | bytes 17825792 | tf_op jit(solution)/reshape | solution.py:58
  394.0 25.9 %collective-permute-start.18 = (f32[512,512]{1,0:T(8,128)}, f32[512,512]{1,0:T(8,128)}, u32[]{:S(2)}, u32[]{:S(2)}) collective-permute-start(f32[512,512]{1,0:T(8,128)} %get-tuple-element.491), channel_id=31, source_target_pairs={{0,1},{1,2},{2,3},{3,4},{4,5},{5,6},{6,7},{7,8},{8,9},{9,10},{10,1... | collective-permute-start | bytes 3145736 | tf_op jit(solution)/vmap(transpose(jvp()))/dot_general | solution.py:9
  603.3 1401.2 %collective-permute-start.28 = (f32[512,512]{1,0:T(8,128)}, f32[512,512]{1,0:T(8,128)}, u32[]{:S(2)}, u32[]{:S(2)}) collective-permute-start(f32[512,512]{1,0:T(8,128)} %get-tuple-element.45), channel_id=32, source_target_pairs={{0,1},{1,2},{2,3},{3,4},{4,5},{5,6},{6,7},{7,8},{8,9},{9,10},{10,1... | collective-permute-start | bytes 3145736 | tf_op jit(solution)/vmap(transpose(jvp()))/dot_general | solution.py:9
  735.6 26.6 %collective-permute-start.22 = (f32[512,512]{0,1:T(8,128)}, f32[512,512]{0,1:T(8,128)}, u32[]{:S(2)}, u32[]{:S(2)}) collective-permute-start(f32[512,512]{0,1:T(8,128)} %get-tuple-element.500), channel_id=37, source_target_pairs={{0,1},{1,2},{2,3},{3,4},{4,5},{5,6},{6,7},{7,8},{8,9},{9,10},{10,1... | collective-permute-start | bytes 3145736 | tf_op jit(solution)/vmap(transpose(jvp()))/dot_general | solution.py:9
  830.3 18.3 collective-permute-start.20
  888.2 18.3 collective-permute-start.20
  944.0 1062.3 %collective-permute-start.29 = (f32[512,512]{0,1:T(8,128)}, f32[512,512]{0,1:T(8,128)}, u32[]{:S(2)}, u32[]{:S(2)}) collective-permute-start(f32[512,512]{0,1:T(8,128)} %get-tuple-element.47), channel_id=38, source_target_pairs={{0,1},{1,2},{2,3},{3,4},{4,5},{5,6},{6,7},{7,8},{8,9},{9,10},{10,1... | collective-permute-start | bytes 3145736 | tf_op jit(solution)/vmap(transpose(jvp()))/dot_general | solution.py:9
  957.3 18.6 collective-permute-start.8
  979.2 34.6 %collective-permute-start.10 = (f32[8192,32]{0,1:T(8,128)}, f32[8192,32]{0,1:T(8,128)}, u32[]{:S(2)}, u32[]{:S(2)}) collective-permute-start(f32[8192,32]{0,1:T(8,128)} %get-tuple-element.473), channel_id=18, source_target_pairs={{0,1},{1,2},{2,3},{3,4},{4,5},{5,6},{6,7},{7,8},{8,9},{9,10},{10,1... | collective-permute-start | bytes 3145736 | tf_op jit(solution)/vmap(transpose(jvp()))/dot_general | solution.py:21
  1019.9 24.3 %collective-permute-start.8 = (f32[8192,32]{0,1:T(8,128)}, f32[8192,32]{0,1:T(8,128)}, u32[]{:S(2)}, u32[]{:S(2)}) collective-permute-start(f32[8192,32]{0,1:T(8,128)} %broadcast_select_fusion.28), channel_id=16, source_target_pairs={{0,1},{1,2},{2,3},{3,4},{4,5},{5,6},{6,7},{7,8},{8,9},{9,10},{10,1... | collective-permute-start | bytes 3145736 | tf_op jit(solution)/vmap(transpose(jvp()))/dot_general | solution.py:21
  1047.6 23.8 %collective-permute-start.10 = (f32[8192,32]{0,1:T(8,128)}, f32[8192,32]{0,1:T(8,128)}, u32[]{:S(2)}, u32[]{:S(2)}) collective-permute-start(f32[8192,32]{0,1:T(8,128)} %get-tuple-element.473), channel_id=18, source_target_pairs={{0,1},{1,2},{2,3},{3,4},{4,5},{5,6},{6,7},{7,8},{8,9},{9,10},{10,1... | collective-permute-start | bytes 3145736 | tf_op jit(solution)/vmap(transpose(jvp()))/dot_general | solution.py:21
  1077.3 25.5 %collective-permute-start.8 = (f32[8192,32]{0,1:T(8,128)}, f32[8192,32]{0,1:T(8,128)}, u32[]{:S(2)}, u32[]{:S(2)}) collective-permute-start(f32[8192,32]{0,1:T(8,128)} %broadcast_select_fusion.28), channel_id=16, source_target_pairs={{0,1},{1,2},{2,3},{3,4},{4,5},{5,6},{6,7},{7,8},{8,9},{9,10},{10,1... | collective-permute-start | bytes 3145736 | tf_op jit(solution)/vmap(transpose(jvp()))/dot_general | solution.py:21
  1106.2 24.1 %collective-permute-start.10 = (f32[8192,32]{0,1:T(8,128)}, f32[8192,32]{0,1:T(8,128)}, u32[]{:S(2)}, u32[]{:S(2)}) collective-permute-start(f32[8192,32]{0,1:T(8,128)} %get-tuple-element.473), channel_id=18, source_target_pairs={{0,1},{1,2},{2,3},{3,4},{4,5},{5,6},{6,7},{7,8},{8,9},{9,10},{10,1... | collective-permute-start | bytes 3145736 | tf_op jit(solution)/vmap(transpose(jvp()))/dot_general | solution.py:21
  1136.3 26.0 %collective-permute-start.8 = (f32[8192,32]{0,1:T(8,128)}, f32[8192,32]{0,1:T(8,128)}, u32[]{:S(2)}, u32[]{:S(2)}) collective-permute-start(f32[8192,32]{0,1:T(8,128)} %broadcast_select_fusion.28), channel_id=16, source_target_pairs={{0,1},{1,2},{2,3},{3,4},{4,5},{5,6},{6,7},{7,8},{8,9},{9,10},{10,1... | collective-permute-start | bytes 3145736 | tf_op jit(solution)/vmap(transpose(jvp()))/dot_general | solution.py:21
  1165.7 24.1 %collective-permute-start.10 = (f32[8192,32]{0,1:T(8,128)}, f32[8192,32]{0,1:T(8,128)}, u32[]{:S(2)}, u32[]{:S(2)}) collective-permute-start(f32[8192,32]{0,1:T(8,128)} %get-tuple-element.473), channel_id=18, source_target_pairs={{0,1},{1,2},{2,3},{3,4},{4,5},{5,6},{6,7},{7,8},{8,9},{9,10},{10,1... | collective-permute-start | bytes 3145736 | tf_op jit(solution)/vmap(transpose(jvp()))/dot_general | solution.py:21
  1193.5 815.8 %collective-permute-start.26 = (f32[8192,32]{0,1:T(8,128)}, f32[8192,32]{0,1:T(8,128)}, u32[]{:S(2)}, u32[]{:S(2)}) collective-permute-start(f32[8192,32]{0,1:T(8,128)} %get-tuple-element.41), channel_id=19, source_target_pairs={{0,1},{1,2},{2,3},{3,4},{4,5},{5,6},{6,7},{7,8},{8,9},{9,10},{10,1... | collective-permute-start | bytes 3145736 | tf_op jit(solution)/vmap(transpose(jvp()))/dot_general | solution.py:21
  1281.6 19.5 collective-permute-start.12
  1304.5 22.5 collective-permute-start.14
  1333.5 27.4 %collective-permute-start.12 = (f32[8192,32]{0,1:T(8,128)}, f32[8192,32]{0,1:T(8,128)}, u32[]{:S(2)}, u32[]{:S(2)}) collective-permute-start(f32[8192,32]{0,1:T(8,128)} %broadcast_select_fusion.30), channel_id=22, source_target_pairs={{0,1},{1,2},{2,3},{3,4},{4,5},{5,6},{6,7},{7,8},{8,9},{9,10},{10,1... | collective-permute-start | bytes 3145736 | tf_op jit(solution)/vmap(transpose(jvp()))/dot_general | solution.py:21
  1364.4 22.5 collective-permute-start.14
  1393.4 29.8 %collective-permute-start.12 = (f32[8192,32]{0,1:T(8,128)}, f32[8192,32]{0,1:T(8,128)}, u32[]{:S(2)}, u32[]{:S(2)}) collective-permute-start(f32[8192,32]{0,1:T(8,128)} %broadcast_select_fusion.30), channel_id=22, source_target_pairs={{0,1},{1,2},{2,3},{3,4},{4,5},{5,6},{6,7},{7,8},{8,9},{9,10},{10,1... | collective-permute-start | bytes 3145736 | tf_op jit(solution)/vmap(transpose(jvp()))/dot_general | solution.py:21
  1398.1 25.2 %collective-permute-start.13 = (f32[8192,32]{0,1:T(8,128)}, f32[8192,32]{0,1:T(8,128)S(1)}, u32[]{:S(2)}, u32[]{:S(2)}) collective-permute-start(f32[8192,32]{0,1:T(8,128)} %broadcast_select_fusion.31), channel_id=21, source_target_pairs={{0,15},{1,0},{2,1},{3,2},{4,3},{5,4},{6,5},{7,6},{8,7},{9,8},{10,9... | collective-permute-start | bytes 3145736 | tf_op jit(solution)/vmap(transpose(jvp()))/dot_general | solution.py:21
  1426.6 22.2 collective-permute-start.14
  1455.4 30.1 %collective-permute-start.12 = (f32[8192,32]{0,1:T(8,128)}, f32[8192,32]{0,1:T(8,128)}, u32[]{:S(2)}, u32[]{:S(2)}) collective-permute-start(f32[8192,32]{0,1:T(8,128)} %broadcast_select_fusion.30), channel_id=22, source_target_pairs={{0,1},{1,2},{2,3},{3,4},{4,5},{5,6},{6,7},{7,8},{8,9},{9,10},{10,1... | collective-permute-start | bytes 3145736 | tf_op jit(solution)/vmap(transpose(jvp()))/dot_general | solution.py:21
  1460.4 25.2 %collective-permute-start.13 = (f32[8192,32]{0,1:T(8,128)}, f32[8192,32]{0,1:T(8,128)S(1)}, u32[]{:S(2)}, u32[]{:S(2)}) collective-permute-start(f32[8192,32]{0,1:T(8,128)} %broadcast_select_fusion.31), channel_id=21, source_target_pairs={{0,15},{1,0},{2,1},{3,2},{4,3},{5,4},{6,5},{7,6},{8,7},{9,8},{10,9... | collective-permute-start | bytes 3145736 | tf_op jit(solution)/vmap(transpose(jvp()))/dot_general | solution.py:21
  1488.9 22.2 collective-permute-start.14
  1517.7 33.2 %collective-permute-start = (f32[8192,32]{0,1:T(8,128)}, f32[8192,32]{0,1:T(8,128)}, u32[]{:S(2)}, u32[]{:S(2)}) collective-permute-start(f32[8192,32]{0,1:T(8,128)} %broadcast_select_fusion.24), channel_id=3, source_target_pairs={{0,1},{1,2},{2,3},{3,4},{4,5},{5,6},{6,7},{7,8},{8,9},{9,10},{10,1... | collective-permute-start | bytes 3145736 | tf_op jit(solution)/vmap(transpose(jvp()))/dot_general | solution.py:20
  1522.6 28.2 %collective-permute-start.1 = (f32[8192,32]{0,1:T(8,128)}, f32[8192,32]{0,1:T(8,128)}, u32[]{:S(2)}, u32[]{:S(2)}) collective-permute-start(f32[8192,32]{0,1:T(8,128)} %broadcast_select_fusion.25), channel_id=2, source_target_pairs={{0,15},{1,0},{2,1},{3,2},{4,3},{5,4},{6,5},{7,6},{8,7},{9,8},{10,9... | collective-permute-start | bytes 3145736 | tf_op jit(solution)/vmap(transpose(jvp()))/dot_general | solution.py:20
  1554.7 19.0 collective-permute-start.2
  1579.7 28.3 %collective-permute-start = (f32[8192,32]{0,1:T(8,128)}, f32[8192,32]{0,1:T(8,128)}, u32[]{:S(2)}, u32[]{:S(2)}) collective-permute-start(f32[8192,32]{0,1:T(8,128)} %broadcast_select_fusion.24), channel_id=3, source_target_pairs={{0,1},{1,2},{2,3},{3,4},{4,5},{5,6},{6,7},{7,8},{8,9},{9,10},{10,1... | collective-permute-start | bytes 3145736 | tf_op jit(solution)/vmap(transpose(jvp()))/dot_general | solution.py:20
  1611.8 20.0 collective-permute-start.2
  1637.7 30.8 %collective-permute-start = (f32[8192,32]{0,1:T(8,128)}, f32[8192,32]{0,1:T(8,128)}, u32[]{:S(2)}, u32[]{:S(2)}) collective-permute-start(f32[8192,32]{0,1:T(8,128)} %broadcast_select_fusion.24), channel_id=3, source_target_pairs={{0,1},{1,2},{2,3},{3,4},{4,5},{5,6},{6,7},{7,8},{8,9},{9,10},{10,1... | collective-permute-start | bytes 3145736 | tf_op jit(solution)/vmap(transpose(jvp()))/dot_general | solution.py:20
  1650.6 18.0 collective-permute-start.1
  1672.4 20.0 collective-permute-start.2
  1698.3 28.6 %collective-permute-start = (f32[8192,32]{0,1:T(8,128)}, f32[8192,32]{0,1:T(8,128)}, u32[]{:S(2)}, u32[]{:S(2)}) collective-permute-start(f32[8192,32]{0,1:T(8,128)} %broadcast_select_fusion.24), channel_id=3, source_target_pairs={{0,1},{1,2},{2,3},{3,4},{4,5},{5,6},{6,7},{7,8},{8,9},{9,10},{10,1... | collective-permute-start | bytes 3145736 | tf_op jit(solution)/vmap(transpose(jvp()))/dot_general | solution.py:20
  1730.8 20.0 collective-permute-start.2
  1756.0 26.3 %collective-permute-start.4 = (f32[8192,32]{0,1:T(8,128)}, f32[8192,32]{0,1:T(8,128)}, u32[]{:S(2)}, u32[]{:S(2)}) collective-permute-start(f32[8192,32]{0,1:T(8,128)} %broadcast_select_fusion.26), channel_id=9, source_target_pairs={{0,1},{1,2},{2,3},{3,4},{4,5},{5,6},{6,7},{7,8},{8,9},{9,10},{10,1... | collective-permute-start | bytes 3145736 | tf_op jit(solution)/vmap(transpose(jvp()))/dot_general | solution.py:20
  1785.8 23.2 collective-permute-start.6
  1815.5 25.5 %collective-permute-start.4 = (f32[8192,32]{0,1:T(8,128)}, f32[8192,32]{0,1:T(8,128)}, u32[]{:S(2)}, u32[]{:S(2)}) collective-permute-start(f32[8192,32]{0,1:T(8,128)} %broadcast_select_fusion.26), channel_id=9, source_target_pairs={{0,1},{1,2},{2,3},{3,4},{4,5},{5,6},{6,7},{7,8},{8,9},{9,10},{10,1... | collective-permute-start | bytes 3145736 | tf_op jit(solution)/vmap(transpose(jvp()))/dot_general | solution.py:20
  1844.4 24.4 %collective-permute-start.6 = (f32[8192,32]{0,1:T(8,128)}, f32[8192,32]{0,1:T(8,128)S(1)}, u32[]{:S(2)}, u32[]{:S(2)}) collective-permute-start(f32[8192,32]{0,1:T(8,128)} %get-tuple-element.464), channel_id=11, source_target_pairs={{0,1},{1,2},{2,3},{3,4},{4,5},{5,6},{6,7},{7,8},{8,9},{9,10},{10,1... | collective-permute-start | bytes 3145736 | tf_op jit(solution)/vmap(transpose(jvp()))/dot_general | solution.py:20
  1875.3 25.5 %collective-permute-start.4 = (f32[8192,32]{0,1:T(8,128)}, f32[8192,32]{0,1:T(8,128)}, u32[]{:S(2)}, u32[]{:S(2)}) collective-permute-start(f32[8192,32]{0,1:T(8,128)} %broadcast_select_fusion.26), channel_id=9, source_target_pairs={{0,1},{1,2},{2,3},{3,4},{4,5},{5,6},{6,7},{7,8},{8,9},{9,10},{10,1... | collective-permute-start | bytes 3145736 | tf_op jit(solution)/vmap(transpose(jvp()))/dot_general | solution.py:20
  1904.2 24.1 %collective-permute-start.6 = (f32[8192,32]{0,1:T(8,128)}, f32[8192,32]{0,1:T(8,128)S(1)}, u32[]{:S(2)}, u32[]{:S(2)}) collective-permute-start(f32[8192,32]{0,1:T(8,128)} %get-tuple-element.464), channel_id=11, source_target_pairs={{0,1},{1,2},{2,3},{3,4},{4,5},{5,6},{6,7},{7,8},{8,9},{9,10},{10,1... | collective-permute-start | bytes 3145736 | tf_op jit(solution)/vmap(transpose(jvp()))/dot_general | solution.py:20
  1934.9 25.5 %collective-permute-start.4 = (f32[8192,32]{0,1:T(8,128)}, f32[8192,32]{0,1:T(8,128)}, u32[]{:S(2)}, u32[]{:S(2)}) collective-permute-start(f32[8192,32]{0,1:T(8,128)} %broadcast_select_fusion.26), channel_id=9, source_target_pairs={{0,1},{1,2},{2,3},{3,4},{4,5},{5,6},{6,7},{7,8},{8,9},{9,10},{10,1... | collective-permute-start | bytes 3145736 | tf_op jit(solution)/vmap(transpose(jvp()))/dot_general | solution.py:20
  1963.7 24.4 %collective-permute-start.6 = (f32[8192,32]{0,1:T(8,128)}, f32[8192,32]{0,1:T(8,128)S(1)}, u32[]{:S(2)}, u32[]{:S(2)}) collective-permute-start(f32[8192,32]{0,1:T(8,128)} %get-tuple-element.464), channel_id=11, source_target_pairs={{0,1},{1,2},{2,3},{3,4},{4,5},{5,6},{6,7},{7,8},{8,9},{9,10},{10,1... | collective-permute-start | bytes 3145736 | tf_op jit(solution)/vmap(transpose(jvp()))/dot_general | solution.py:20
  1992.4 18.2 collective-permute-start.27
  2004.4 26.5 %collective-permute-start.25 = (f32[8192,32]{0,1:T(8,128)}, f32[8192,32]{0,1:T(8,128)S(1)}, u32[]{:S(2)}, u32[]{:S(2)}) collective-permute-start(f32[8192,32]{0,1:T(8,128)} %get-tuple-element.39), channel_id=12, source_target_pairs={{0,1},{1,2},{2,3},{3,4},{4,5},{5,6},{6,7},{7,8},{8,9},{9,10},{10,1... | collective-permute-start | bytes 3145736 | tf_op jit(solution)/vmap(transpose(jvp()))/dot_general | solution.py:20
  2082.5 155.9 %all-gather.12.cloned.1.call-start = ((), (), s32[]{:S(2)}) async-start(), calls=%async_computation.1 | async-start | bytes 17825792 | tf_op jit(solution)/reshape | solution.py:58
  2088.7 228.6 %all-gather.10.cloned.1.call-start = ((), (), s32[]{:S(2)}) async-start(), calls=%async_computation | async-start | bytes 17825792 | tf_op jit(solution)/reshape | solution.py:58
  (101 other events, 2012.5 us)
Sparse Core Ops, SparseCore 0:
  2082.6 76.8 all-gather.13
  2162.4 76.0 all-gather.11
  2241.3 76.0 all-gather.9
where the time goes:
time: 2370 us; the launch traced here: 2360 us
  matrix products  955 us (40%)
  starting transfers between devices  524 us (22%)
  waiting for transfers between devices  360 us (15%)
  other arithmetic  324 us (14%)
  local copies, waits for them, and re-layouts  136 us (6%)
  blocking collectives  40.6 us (2%)
    dot_general x19, matrix products, layer(): gate = jnp.dot(a, w['w_gate'], preferred_element_type=jnp.float32)  394 us
    dot_general x19, matrix products, layer(): up = jnp.dot(a, w['w_up'], preferred_element_type=jnp.float32)  355 us
    reshape x3, waiting for transfers between devices, step(): t.reshape(-1, *t.shape[2:])  223 us
    dot_general x34, starting transfers between devices, matmul(): jnp.dot(a, w, preferred_element_type=jnp.float32).astype(jnp.bfloat16)  215 us
    dot_general x19, matrix products, matmul(): jnp.dot(a, w, preferred_element_type=jnp.float32).astype(jnp.bfloat16)  206 us
    dot_general x34, starting transfers between devices, layer(): up = jnp.dot(a, w['w_up'], preferred_element_type=jnp.float32)  169 us
    dot_general x34, starting transfers between devices, layer(): gate = jnp.dot(a, w['w_gate'], preferred_element_type=jnp.float32)  139 us
    unnamed x72, local copies, waits for them, and re-layouts  129 us
  transfers between devices with their start and end apart: 105, of which 23 were waited for; matrix products, arithmetic and copies ran while one was open for 41% of the time, Pallas kernels for 0%

commit v1 on v0

v1 whole, which is shorter than its diff:
```python
import functools
import jax, jax.numpy as jnp
from jax import lax
from jax.experimental import pallas as pl
from jax.experimental.pallas import tpu as pltpu

T, D, FF = 2048, 512, 8192
C = 512
NT = (((1,), (1,)), ((), ()))

def dot(a, b):
    return jnp.dot(a, b, preferred_element_type=jnp.float32)

def dot_nt(a, b):
    return lax.dot_general(a, b, NT, preferred_element_type=jnp.float32)

def norm_to(h_ref, a_ref):
    wide = h_ref[...].astype(jnp.float32)
    scale = lax.rsqrt(jnp.mean(wide * wide, -1, keepdims=True) + 1e-6)
    a_ref[...] = (wide * scale).astype(jnp.bfloat16)

def fwd_kernel(x, wg, wu, wd, h1, a_s, acc):
    k = pl.program_id(0)

    @pl.when(k == 0)
    def _():
        norm_to(x, a_s)
        acc[...] = jnp.zeros_like(acc)

    def chunk(c, _):
        rows = pl.ds(pl.multiple_of(c * C, C), C)
        a = a_s[rows, :]
        gate = dot(a, wg[0])
        up = dot(a, wu[0])
        act = (gate * jax.nn.sigmoid(gate) * up).astype(jnp.bfloat16)
        acc[rows, :] += dot(act, wd[0])
        return 0

    lax.fori_loop(0, T // C, chunk, 0)

    @pl.when(k == pl.num_programs(0) - 1)
    def _():
        h1[...] = x[...] + acc[...].astype(jnp.bfloat16)

def forward(x, wg, wu, wd, layer, F=512):
    return pl.pallas_call(
        fwd_kernel,
        grid=(FF // F,),
        in_specs=[
            pl.BlockSpec((T, D), lambda k: (0, 0)),
            pl.BlockSpec((1, D, F), lambda k: (layer, 0, k)),
            pl.BlockSpec((1, D, F), lambda k: (layer, 0, k)),
            pl.BlockSpec((1, F, D), lambda k: (layer, k, 0)),
        ],
        out_specs=pl.BlockSpec((T, D), lambda k: (0, 0)),
        out_shape=jax.ShapeDtypeStruct((T, D), jnp.bfloat16),
        scratch_shapes=[pltpu.VMEM((T, D), jnp.bfloat16), pltpu.VMEM((T, D), jnp.float32)],
        cost_estimate=pl.CostEstimate(flops=6 * T * D * FF, bytes_accessed=3 * D * FF * 2, transcendentals=0),
        compiler_params=pltpu.CompilerParams(vmem_limit_bytes=56 << 20, dimension_semantics=("arbitrary",)),
    )(x, wg, wu, wd)

MESH = pl.DeviceIdType.MESH
ORDERS = ((0, 1, 2), (1, 2, 0), (2, 0, 1))

def place():
    me = lax.axis_index("dp")
    return me, [me // bit % 2 for bit in (8, 4, 2, 1)]

def other(me, mask):
    for bit in (8, 4, 2, 1):
        if mask & bit:
            me = me + bit * (1 - 2 * (me // bit % 2))
    return me

def greet(masks):
    me, _ = place()
    barrier = pltpu.get_barrier_semaphore()
    for mask in masks:
        pl.semaphore_signal(barrier, inc=1, device_id={"dp": other(me, mask)}, device_id_type=MESH)
    pl.semaphore_wait(barrier, len(masks))

def rs_scratch(S):
    vm = lambda *lead: pltpu.VMEM(lead + (256, 512), jnp.bfloat16)
    per = [vm(2, 2, 2), vm(2, 2, 2), vm(2, 2), vm(2), vm()]
    return per * 3 + [pltpu.SemaphoreType.DMA((3, S)), pltpu.SemaphoreType.DMA((4, 3, S)), pltpu.SemaphoreType.DMA((4, 3, S))]
RS_REFS = 18

class Scatter:
    def __init__(self, g, refs, S):
        self.g, self.S, self.R = g, S, 256 // S
        self.buf = [refs[5 * p : 5 * p + 5] for p in range(3)]
        self.loc, self.snd, self.rcv = refs[15:18]
        self.me, self.at = place()

    def rows(self, s):
        return pl.ds(s * self.R, self.R)

    def copy(self, step, p, s):
        own = self.buf[p][0]
        rows = self.rows(s)
        if step == 0:
            src, bit = self.g[p].at[:, :, :, 1 - self.at[3], rows], 1
        else:
            order = ORDERS[p]
            index = [slice(None)] * 3
            for axis in order[: step - 1]:
                index[axis] = self.at[axis]
            index[order[step - 1]] = 1 - self.at[order[step - 1]]
            src, bit = own.at[(*index, rows)], 8 >> order[step - 1]
        into = self.buf[p][step + 1]
        dst = into.at[(slice(None),) * (len(into.shape) - 2) + (rows,)]
        return pltpu.make_async_remote_copy(
            src_ref=src, dst_ref=dst, send_sem=self.snd.at[step, p, s], recv_sem=self.rcv.at[step, p, s],
            device_id={"dp": other(self.me, bit)}, device_id_type=MESH)

    def local(self, p, s):
        rows = self.rows(s)
        return pltpu.make_async_copy(self.g[p].at[:, :, :, self.at[3], rows], self.buf[p][0].at[:, :, :, rows], self.loc.at[p, s])

    def summed(self, p, upto, index, rows):
        order = ORDERS[p]
        total = self.buf[p][0][(*index, rows, slice(None))].astype(jnp.float32)
        total += self.buf[p][1][(*index, rows, slice(None))].astype(jnp.float32)
        for n in range(1, upto):
            left = sorted(order[n:])
            total += self.buf[p][n + 1][(*[index[axis] for axis in left], rows, slice(None))].astype(jnp.float32)
        return total

    def start(self, s):
        for p in range(3):
            self.copy(0, p, s).start()
            self.local(p, s).start()

    def advance(self, step, s):
        for p in range(3):
            order = ORDERS[p]
            if step == 1:
                self.local(p, s).wait()
            self.copy(step - 1, p, s).wait_recv()
            free = order[step:]

            def block(i, _):
                index = [None] * 3
                for axis in order[: step - 1]:
                    index[axis] = self.at[axis]
                index[order[step - 1]] = 1 - self.at[order[step - 1]]
                n = i // max(1, self.R // 64)
                for axis in free:
                    index[axis] = n % 2
                    n = n // 2
                small = min(64, self.R)
                rows = pl.ds(pl.multiple_of(s * self.R + i % (self.R // small) * small, small), small)
                self.buf[p][0][(*index, rows, slice(None))] = self.summed(p, step, index, rows).astype(jnp.bfloat16)
                return 0

            lax.fori_loop(0, (1 << len(free)) * max(1, self.R // 64), block, 0)
            self.copy(step, p, s).start()

    def finish(self, s, outs):
        for p in range(3):
            self.copy(3, p, s).wait_recv()
            rows = self.rows(s)
            outs[p][rows, :] = self.summed(p, 4, self.at[:3], rows).astype(jnp.bfloat16)
        for step in range(4):
            for p in range(3):
                self.copy(step, p, s).wait_send()

def bwd_kernel(need_da, last, hosts, *refs):
    refs = list(refs)
    h, dh = refs[:2]
    wg, wu, wd = refs[2:4], refs[4:6], refs[6:8]
    refs = refs[8:]
    da_in = refs.pop(0) if need_da and last else None
    if hosts:
        g_in, refs = refs[:3], refs[3:]
    gg, gu, gd = refs[:3]
    refs = refs[3:]
    da_out = refs.pop(0) if need_da else None
    if hosts:
        summed, refs = refs[:3], refs[3:]
    a_s, aT, dhT, dg_s, du_s, act_s = refs[:6]
    refs = refs[6:]
    acc = refs.pop(0) if need_da else None
    da_sem = refs.pop(0) if need_da and last else None
    k = pl.program_id(0)
    if hosts:
        scatter = Scatter(g_in, refs, 1)

        @pl.when(k == 0)
        def _():
            greet((8, 4, 2, 1))
            scatter.start(0)

        for step, when in ((1, 2), (2, 5), (3, 7)):
            @pl.when(k == when)
            def _():
                scatter.advance(step, 0)

    @pl.when(k == 0)
    def _():
        norm_to(h, a_s)
        aT[...] = a_s[...].T
        dhT[...] = dh[...].T
        if need_da:
            if last:
                copy = pltpu.make_async_copy(da_in, acc, da_sem)
                copy.start()
                copy.wait()
            else:
                acc[...] = jnp.zeros_like(acc)

    def chunk(c, _):
        rows = pl.ds(pl.multiple_of(c * C, C), C)
        a = a_s[rows, :]
        dy = dh[rows, :]
        for b in range(2):
            cols = slice(b * 256, b * 256 + 256)
            gate = dot(a, wg[b][0])
            up = dot(a, wu[b][0])
            dact = dot_nt(dy, wd[b][0]).astype(jnp.bfloat16).astype(jnp.float32)
            s = jax.nn.sigmoid(gate)
            silu = gate * s
            act_s[rows, cols] = (silu * up).astype(jnp.bfloat16)
            du_s[rows, cols] = (dact * silu).astype(jnp.bfloat16)
            dg_s[rows, cols] = (dact * up * (s + silu * (1.0 - s))).astype(jnp.bfloat16)
        if need_da:
            t = acc[rows, :]
            for b in range(2):
                cols = slice(b * 256, b * 256 + 256)
                t += dot_nt(dg_s[rows, cols], wg[b][0]) + dot_nt(du_s[rows, cols], wu[b][0])
            acc[rows, :] = t
        return 0

    lax.fori_loop(0, T // C, chunk, 0)
    gg[...] = dot(aT[...], dg_s[...]).astype(jnp.bfloat16).reshape(16, 32, 512)
    gu[...] = dot(aT[...], du_s[...]).astype(jnp.bfloat16).reshape(16, 32, 512)
    gd[...] = dot(dhT[...], act_s[...]).T.astype(jnp.bfloat16).reshape(2, 256, 512)

    if need_da:
        @pl.when(k == pl.num_programs(0) - 1)
        def _():
            if not last:
                da_out[...] = acc[...]
            else:
                wide = h[...].astype(jnp.float32)
                scale = lax.rsqrt(jnp.mean(wide * wide, -1, keepdims=True) + 1e-6)
                da = acc[...].astype(jnp.bfloat16).astype(jnp.float32)
                along = jnp.mean(da * wide, -1, keepdims=True)
                da_out[...] = dh[...] + (da * scale - wide * (scale * scale * scale * along)).astype(jnp.bfloat16)

    if hosts:
        @pl.when(k == pl.num_programs(0) - 1)
        def _():
            scatter.finish(0, summed)

G = jax.ShapeDtypeStruct((16, 256, 512), jnp.bfloat16)
OWN = jax.ShapeDtypeStruct((256, 512), jnp.bfloat16)

def backward(h, dh, wg, wu, wd, layer, half, need_da, da=None, g=None, number=None):
    last = da is not None
    hosts = g is not None
    whole = pl.BlockSpec((T, D), lambda k: (0, 0), pipeline_mode=pl.Buffered(1))
    wide = [pl.BlockSpec((1, D, 256), lambda k, b=b: (layer, 0, (2 * k + b) * 2 + half)) for b in range(2)]
    tall = [pl.BlockSpec((1, 256, D), lambda k, b=b: (layer, (2 * k + b) * 2 + half, 0)) for b in range(2)]
    outs = [G, G, G]
    out_specs = [pl.BlockSpec((16, 32, 512), lambda k: (0, k, 0))] * 2 + [pl.BlockSpec((2, 256, 512), lambda k: (k, 0, 0))]
    scratch = [pltpu.VMEM((T, D), jnp.bfloat16), pltpu.VMEM((D, T), jnp.bfloat16), pltpu.VMEM((D, T), jnp.bfloat16)]
    scratch += [pltpu.VMEM((T, 512), jnp.bfloat16)] * 3
    args = [h, dh, wg, wg, wu, wu, wd, wd]
    in_specs = [whole, whole] + wide * 2 + tall
    if need_da:
        outs.append(jax.ShapeDtypeStruct((T, D), jnp.bfloat16 if last else jnp.float32))
        out_specs.append(whole)
        scratch.append(pltpu.VMEM((T, D), jnp.float32))
        if last:
            args.append(da)
            in_specs.append(pl.BlockSpec(memory_space=pl.ANY))
            scratch.append(pltpu.SemaphoreType.DMA)
    params = {}
    if hosts:
        args += [t.reshape(2, 2, 2, 2, 256, 512) for t in g]
        in_specs += [pl.BlockSpec(memory_space=pl.ANY)] * 3
        outs += [OWN] * 3
        out_specs += [pl.BlockSpec((256, 512), lambda k: (0, 0))] * 3
        scratch += rs_scratch(1)
        params = {"collective_id": number, "has_side_effects": True}
    out = pl.pallas_call(
        functools.partial(bwd_kernel, need_da, last, hosts),
        grid=(8,),
        in_specs=in_specs,
        out_specs=out_specs,
        out_shape=outs,
        scratch_shapes=scratch,
        cost_estimate=pl.CostEstimate(flops=(16 if need_da else 12) * T * D * FF // 2, bytes_accessed=3 * D * FF * 2, transcendentals=0),
        compiler_params=pltpu.CompilerParams(vmem_limit_bytes=62 << 20, dimension_semantics=("arbitrary",), **params),
    )(*args)
    return out[:3], (out[3] if need_da else None), (out[-3:] if hosts else None)

TAIL = 4

def tail_kernel(*refs):
    g_in, done, (a, b, c, total), refs = refs[:3], refs[3:12], refs[12:16], refs[16:]
    scatter = Scatter(g_in, refs[:RS_REFS], TAIL)
    parts, snd, rcv = refs[RS_REFS:]
    me, _ = place()
    greet(range(1, 16))
    for t in range(TAIL + 4):
        for step in range(4, -1, -1):
            s = t - step
            if 0 <= s < TAIL:
                if step == 0:
                    scatter.start(s)
                elif step < 4:
                    scatter.advance(step, s)
                else:
                    scatter.finish(s, (a, b, c))
    square = jnp.zeros((1, 512), jnp.float32)
    for ref in (*done, a, b, c):
        wide = ref[...].astype(jnp.float32)
        square += jnp.sum(wide * wide, 0, keepdims=True)
    square = square[:, :128] + square[:, 128:256] + square[:, 256:384] + square[:, 384:]
    parts[me] = jnp.broadcast_to(square, (8, 128))
    copies = [
        pltpu.make_async_remote_copy(
            src_ref=parts.at[me], dst_ref=parts.at[me], send_sem=snd.at[mask], recv_sem=rcv.at[mask],
            device_id={"dp": other(me, mask)}, device_id_type=MESH)
        for mask in range(1, 16)
    ]
    for copy in copies:
        copy.start()
    for copy in copies:
        copy.wait()
    whole = jnp.sum(parts[...], 0)
    total[...] = jnp.broadcast_to(jnp.sum(whole, 1, keepdims=True), (8, 128))

def tail(g, done):
    return pl.pallas_call(
        tail_kernel,
        in_specs=[pl.BlockSpec(memory_space=pl.ANY)] * 3 + [pl.BlockSpec(memory_space=pltpu.VMEM)] * 9,
        out_specs=[pl.BlockSpec(memory_space=pltpu.VMEM)] * 4,
        out_shape=[OWN] * 3 + [jax.ShapeDtypeStruct((8, 128), jnp.float32)],
        scratch_shapes=rs_scratch(TAIL) + [pltpu.VMEM((16, 8, 128), jnp.float32), pltpu.SemaphoreType.DMA((16,)), pltpu.SemaphoreType.DMA((16,))],
        compiler_params=pltpu.CompilerParams(vmem_limit_bytes=48 << 20, collective_id=4, has_side_effects=True),
    )(*[t.reshape(2, 2, 2, 2, 256, 512) for t in g], *done)

def update_kernel(me, total, *refs):
    g, (ws, ms, vs), outs = refs[:12], (refs[12:15], refs[15:18], refs[18:21]), refs[21:]
    factor = jnp.minimum(1.0, 0.5 * lax.rsqrt(total[0:1, 0:1] / (3 * 2 * D * FF) + 1e-30))
    k = pl.program_id(0)

    def one(i, at, grad):
        grad = grad.astype(jnp.float32) * factor
        m = 0.9 * ms[i][at] + 0.1 * grad
        v = 0.95 * vs[i][at] + 0.05 * grad * grad
        w = ws[i][at].astype(jnp.float32)
        outs[i][at] = (w - 0.02 * (m * lax.rsqrt(v + 1e-8) + 0.1 * w)).astype(jnp.bfloat16)
        outs[3 + i][at] = m
        outs[6 + i][at] = v

    for layer in range(2):
        for half in range(2):
            for i in range(2):
                for b in range(2):
                    grad = g[(layer * 2 + half) * 3 + i][:, b * 256 : b * 256 + 256]
                    one(i, (layer, slice(None), slice(b * 512 + half * 256, b * 512 + half * 256 + 256)), grad)

            @pl.when(k // 4 == half)
            def _():
                one(2, (layer,), g[(layer * 2 + half) * 3 + 2][...])

def update(me, total, g, w, m, v):
    wide = pl.BlockSpec((2, 32, 1024), lambda k, me: (0, 0, k))
    tall = pl.BlockSpec((2, 64, 512), lambda k, me: (0, k, 0))
    state = [wide, wide, tall]
    weights = [pl.BlockSpec((2, 32, 1024), lambda k, me: (0, me[0], k))] * 2 + [pl.BlockSpec((2, 64, 512), lambda k, me: (0, me[0] * 8 + k, 0))]
    grads = ([pl.BlockSpec((32, 512), lambda k, me: (k, 0))] * 2 + [pl.BlockSpec((64, 512), lambda k, me: (k % 4, 0))]) * 4
    shapes = [(2, 32, FF), (2, 32, FF), (2, 512, D)]
    return pl.pallas_call(
        update_kernel,
        grid_spec=pltpu.PrefetchScalarGridSpec(
            num_scalar_prefetch=1,
            grid=(8,),
            in_specs=[pl.BlockSpec((8, 128), lambda k, me: (0, 0))] + grads + weights + state + state,
            out_specs=state * 3,
        ),
        out_shape=[jax.ShapeDtypeStruct(s, t) for t in (jnp.bfloat16, jnp.float32, jnp.float32) for s in shapes],
        compiler_params=pltpu.CompilerParams(vmem_limit_bytes=48 << 20, dimension_semantics=("arbitrary",)),
    )(me.reshape(1), total, *g, *w, *m, *v)

def gather_kernel(*refs):
    own, full, (loc, snd, rcv, csnd, crcv) = refs[:3], refs[3:6], refs[6:]
    me, at = place()
    greet((8, 4, 2, 1))

    def block(p, layer, number):
        n = full[p].shape[1] // 16
        return full[p].at[layer, pl.ds(pl.multiple_of(number * n, n), n)]

    def send(p, layer, number, slot, bit, sems):
        src = own[p].at[layer] if number is me else block(p, layer, number)
        copy = pltpu.make_async_remote_copy(
            src_ref=src, dst_ref=block(p, layer, number), send_sem=sems[0].at[p, layer, slot], recv_sem=sems[1].at[p, layer, slot],
            device_id={"dp": other(me, bit)}, device_id_type=MESH)
        copy.start()
        sent.append(copy)

    def arrived(p, layer, number, slot, sems):
        pltpu.make_async_remote_copy(
            src_ref=block(p, layer, number), dst_ref=block(p, layer, number), send_sem=sems[0].at[p, layer, slot],
            recv_sem=sems[1].at[p, layer, slot], device_id={"dp": other(me, 1)}, device_id_type=MESH).wait_recv()

    sent = []
    ici, core = (snd, rcv), (csnd, crcv)
    bits = [[8 >> axis for axis in order] for order in ORDERS]
    each = [(p, layer) for layer in range(2) for p in range(3)]
    local = [pltpu.make_async_copy(own[p].at[layer], block(p, layer, me), loc.at[p, layer]) for p, layer in each]
    for step in range(3):
        for p, layer in each:
            send(p, layer, me, 1 << step, bits[p][step], ici)
    for p, layer in each:
        send(p, layer, me, 0, 1, core)
    for copy in local:
        copy.start()
    for step in range(3):
        for slot in range(1 << step, 2 << step):
            for p, layer in each:
                mask = sum(bits[p][i] for i in range(3) if slot >> i & 1)
                number = other(me, mask)
                arrived(p, layer, number, slot, ici)
                for later in range(step + 1, 3):
                    send(p, layer, number, slot | 1 << later, bits[p][later], ici)
                send(p, layer, number, slot, 1, core)
    for slot in range(8):
        for p, layer in each:
            mask = sum(bits[p][i] for i in range(3) if slot >> i & 1)
            arrived(p, layer, other(me, mask + 1), slot, core)
    for copy in local:
        copy.wait()
    for copy in sent:
        copy.wait_send()

def gather(new):
    sems = lambda n: pltpu.SemaphoreType.DMA((3, 2, n))
    return pl.pallas_call(
        gather_kernel,
        in_specs=[pl.BlockSpec(memory_space=pltpu.VMEM)] * 3,
        out_specs=[pl.BlockSpec(memory_space=pl.ANY)] * 3,
        out_shape=[jax.ShapeDtypeStruct((2, t.shape[1] * 16, t.shape[2]), t.dtype) for t in new],
        scratch_shapes=[pltpu.SemaphoreType.DMA((3, 2)), sems(8), sems(8), sems(8), sems(8)],
        compiler_params=pltpu.CompilerParams(vmem_limit_bytes=32 << 20, collective_id=5, has_side_effects=True),
    )(*new)

def solution(mesh):
    P = jax.sharding.PartitionSpec
    rows = P(None, "dp", None)

    def step(x, dy, *arrays):
        x, dy = x[0], dy[0]
        w, m, v = (arrays[i : i + 3] for i in (0, 3, 6))
        h1 = forward(x, *w, 0)
        g1a, da, _ = backward(h1, dy, *w, 1, 0, True)
        g1b, dh, s1a = backward(h1, dy, *w, 1, 1, True, da=da, g=g1a, number=1)
        g0a, _, s1b = backward(x, dh, *w, 0, 0, False, g=g1b, number=2)
        g0b, _, s0a = backward(x, dh, *w, 0, 1, False, g=g0a, number=3)
        *s0b, total = tail(g0b, [*s1a, *s1b, *s0a])
        new = update(lax.axis_index("dp"), total, [*s0a, *s0b, *s1a, *s1b], w, m, v)
        return (*gather(new[:3]), *new[3:])

    return jax.shard_map(
        step,
        mesh=mesh,
        in_specs=(P(("rep", "dp")),) * 2 + (P(),) * 3 + (rows,) * 6,
        out_specs=(P("rep"),) * 3 + (P("rep", "dp"),) * 6,
        check_vma=False,
    )
```

time: 2370 us -> 673 us (0.28)
  matrix products: 955 us -> 0 us
  Pallas kernels: 0 us -> 638 us
  starting transfers between devices: 524 us -> 0 us
  waiting for transfers between devices: 360 us -> 0 us
  other arithmetic: 324 us -> 0.01 us
  local copies, waits for them, and re-layouts: 136 us -> 33.9 us
  blocking collectives: 40.6 us -> 0 us
    dot_general x57 -> x0, matrix products: 955 us -> none  [the longest x19 394 us: layer(): gate = jnp.dot(a, w['w_gate'], preferred_element_type=jnp.float32)]
    pallas_call x0 -> x8, Pallas kernels: none -> 638 us  [the longest x4 333 us: backward(): pl.pallas_call(functools.partial(bwd_kernel, need_da, last, hosts), grid=...]
    dot_general x102 -> x0, starting transfers between devices: 523 us -> none  [the longest x34 215 us: matmul(): jnp.dot(a, w, preferred_element_type=jnp.float32).astype(jnp.bfloat16)]
    dot_general x96 -> x0, other arithmetic: 236 us -> none
    reshape x3 -> x0, waiting for transfers between devices: 223 us -> none  [step(): t.reshape(-1, *t.shape[2:])]
    dot_general x102 -> x0, waiting for transfers between devices: 137 us -> none  [the longest x34 119 us: matmul(): jnp.dot(a, w, preferred_element_type=jnp.float32).astype(jnp.bfloat16)]
    unnamed x72 -> x31, local copies, waits for them, and re-layouts: 129 us -> 33.9 us
    convert_element_type x3 -> x0, other arithmetic: 56.6 us -> none  [the longest x1 52.5 us: layer(): (jax.nn.silu(gate) * up).astype(jnp.bfloat16)]
  transfers between devices with their start and end apart: 105 -> 0, of which waited for: 23 -> 0; matrix products, arithmetic and copies ran while one was open for 41% -> 0% of each run, Pallas kernels for 0% -> 0%
where the time goes in v1:
time: 673 us
  Pallas kernels  638 us (95%)
  local copies, waits for them, and re-layouts  33.9 us (5%)
    pallas_call x4, Pallas kernels, backward(): pl.pallas_call(functools.partial(bwd_kernel, need_da, last, hosts), grid=...  333 us
    pallas_call x1, Pallas kernels, gather(): pl.pallas_call(gather_kernel, in_specs=[pl.BlockSpec(memory_space=pltpu.V...  165 us
    pallas_call x1, Pallas kernels, forward(): pl.pallas_call(fwd_kernel, grid=(FF // F,), in_specs=[pl.BlockSpec((T, D)...  68.4 us
    pallas_call x1, Pallas kernels, tail(): pl.pallas_call(tail_kernel, in_specs=[pl.BlockSpec(memory_space=pl.ANY)]...  57.8 us
    unnamed x31, local copies, waits for them, and re-layouts  33.9 us
    pallas_call x1, Pallas kernels, update(): pl.pallas_call(update_kernel, grid_spec=pltpu.PrefetchScalarGridSpec(num_...  14.1 us

profile of v1, /device:TPU:0, one launch (start us, length us, event | category | flops | bytes accessed | tf_op | source)
XLA Modules:
  0.0 673.0 jit_solution(15659288025393650686)
XLA Ops:
  0.6 68.4 %shard_map.178.refs_0_ = bf16[2048,512]{1,0:T(8,128)(2,1)} custom-call(bf16[2048,512]{1,0:T(8,128)(2,1)} %bitcast.22, bf16[2,512,8192]{2,1,0:T(8,128)(2,1)} %refs_12_.1, bf16[2,512,8192]{2,1,0:T(8,128)(2,1)} %refs_13_.1, bf16[2,8192,512]{2,1,0:T(8,128)(2,1)} %refs_14_.1), custom_call_target="tpu_custom_call" | custom-call | flops 51539607552 | bytes 25165824 | tf_op jit(solution)/shard_map/pallas_call | solution.py:46
  69.0 87.2 %shard_map.179 = (bf16[16,256,512]{2,1,0:T(8,128)(2,1)}, bf16[16,256,512]{2,1,0:T(8,128)(2,1)}, bf16[16,256,512]{2,1,0:T(8,128)(2,1)}, f32[2048,512]{1,0:T(8,128)}) custom-call(bf16[2048,512]{1,0:T(8,128)(2,1)} %shard_map.178.refs_0_, bf16[2048,512]{1,0:T(8,128)(2,1)} %bitcast.20, bf16[2,512,8192]{2,1,0:T(8,128)(2,1)} %refs_12_.1, ...), custom_call_target="tpu_custom_call" | custom-call | flops 68719476736 | bytes 25165824 | tf_op jit(solution)/shard_map/pallas_call | solution.py:287
  156.2 98.4 %shard_map.180 = (bf16[16,256,512]{2,1,0:T(8,128)(2,1)}, bf16[16,256,512]{2,1,0:T(8,128)(2,1)}, bf16[16,256,512]{2,1,0:T(8,128)(2,1)}, bf16[2048,512]{1,0:T(8,12...) custom-call(bf16[2048,512]{1,0:T(8,128)(2,1)} %shard_map.178.refs_0_, ...), custom_call_target="tpu_custom_call" | custom-call | flops 68719476736 | bytes 25165824 | tf_op jit(solution)/shard_map/pallas_call | solution.py:287
  254.6 74.0 %shard_map.181 = (bf16[16,256,512]{2,1,0:T(8,128)(2,1)}, bf16[16,256,512]{2,1,0:T(8,128)(2,1)}, bf16[16,256,512]{2,1,0:T(8,128)(2,1)}, bf16[256,512]{1,0:T(8,128...) custom-call(bf16[2048,512]{1,0:T(8,128)(2,1)} %bitcast.23, bf16[2048,512]{1,0:T(8,128)(2,1)} %get-tuple-element.52.refs_1_, ...), custom_call_target="tpu_custom_call" | custom-call | flops 51539607552 | bytes 25165824 | tf_op jit(solution)/shard_map/pallas_call | solution.py:287
  328.7 0.0 copy-start
  328.7 0.0 copy-start.1
  328.7 0.0 copy-start.2
  328.7 0.0 copy-start.3
  328.7 0.0 copy-start.4
  328.7 0.0 copy-start.5
  328.7 73.4 %shard_map.182 = (bf16[16,256,512]{2,1,0:T(8,128)(2,1)}, bf16[16,256,512]{2,1,0:T(8,128)(2,1)}, bf16[16,256,512]{2,1,0:T(8,128)(2,1)}, bf16[256,512]{1,0:T(8,128...) custom-call(bf16[2048,512]{1,0:T(8,128)(2,1)} %bitcast.24, bf16[2048,512]{1,0:T(8,128)(2,1)} %get-tuple-element.52.refs_1_, ...), custom_call_target="tpu_custom_call" | custom-call | flops 51539607552 | bytes 25165824 | tf_op jit(solution)/shard_map/pallas_call | solution.py:287
  402.2 0.0 copy-done
  402.2 0.0 copy-done.1
  402.2 0.0 copy-done.2
  402.2 0.0 copy-done.3
  402.2 0.0 copy-done.4
  402.2 0.0 copy-done.5
  402.2 0.0 copy-start.6
  402.3 0.9 copy-done.6
  403.2 0.0 copy-start.7
  403.2 0.9 copy-done.7
  404.2 0.0 copy-start.8
  404.2 0.9 copy-done.8
  405.1 57.8 %shard_map.183 = (bf16[256,512]{1,0:T(8,128)(2,1)S(1)}, bf16[256,512]{1,0:T(8,128)(2,1)S(1)}, bf16[256,512]{1,0:T(8,128)(2,1)S(1)}, f32[8,128]{1,0:T(8,128)S(1)}) custom-call(bf16[2,2,2,2,256,512]{5,4,3,2,1,0:T(8,128)(2,1)} %bitcast.17, bf16[2,2,2,2,256,512]{5,4,3,2,1,0:T(8,128)(2,1)} %bitcast.18, bf16[2,2,2,2,256,512]{5,4,3,2,1,0:T(8,128)(2,1)} %bitcast.19, ...), custom_call_target="tpu_custom_call" | custom-call | tf_op jit(solution)/shard_map/pallas_call | solution.py:337
  462.9 14.1 %shard_map.184 = (bf16[2,32,8192]{2,1,0:T(8,128)(2,1)S(1)}, bf16[2,32,8192]{2,1,0:T(8,128)(2,1)S(1)}, bf16[2,512,512]{2,1,0:T(8,128)(2,1)}, f32[2,32,8192]{2,1,0...) custom-call(s32[1]{0:T(128)} %bitcast.me, ...), custom_call_target="tpu_custom_call" | custom-call | tf_op jit(solution)/shard_map/pallas_call | solution.py:378
  477.0 0.0 copy-start.9
  477.0 1.2 copy-done.9
  478.2 164.8 %shard_map.185 = (bf16[2,512,8192]{2,1,0:T(8,128)(2,1)S(1)}, bf16[2,512,8192]{2,1,0:T(8,128)(2,1)}, bf16[2,8192,512]{2,1,0:T(8,128)(2,1)}) custom-call(bf16[2,32,8192]{2,1,0:T(8,128)(2,1)S(1)} %get-tuple-element.75.refs_0_, bf16[2,32,8192]{2,1,0:T(8,128)(2,1)S(1)} %get-tuple-element.76.refs_1_, bf16[2,512,512]{2,1,0:T(8,128)(2,1)S(1)} %copy-done.9), custom_call_target="tpu_custom_call" | custom-call | tf_op jit(solution)/shard_map/pallas_call | solution.py:444
  643.1 0.0 slice-start
  643.1 0.0 slice-start.1
  643.1 8.5 %copy.23 = bf16[2,512,8192]{2,1,0:T(8,128)(2,1)} copy(bf16[2,512,8192]{2,1,0:T(8,128)(2,1)S(1)} %get-tuple-element.96) | data formatting | bytes 33554432
  651.6 0.0 slice-start.2
  651.6 0.0 slice-start.3
  651.6 15.2 %copy.24 = bf16[2,512,8192]{2,1,0:T(8,128)(2,1)} copy(bf16[2,512,8192]{2,1,0:T(8,128)(2,1)} %get-tuple-element.97) | data formatting | bytes 33554432
  666.8 0.0 slice-done
  666.8 0.0 slice-done.1
  666.8 0.0 slice-done.2
  666.8 0.0 slice-done.3
  666.8 6.2 copy.25
  (1 shorter events, 0.0 us)
Async XLA Ops:
  328.7 73.5 %copy-start = (bf16[256,512]{1,0:T(8,128)(2,1)S(1)}, bf16[256,512]{1,0:T(8,128)(2,1)}, u32[]{:S(2)}) copy-start(bf16[256,512]{1,0:T(8,128)(2,1)} %get-tuple-element.62.refs_3_.refs_6_) | copy-start | bytes 786436
  328.7 73.5 %copy-start.1 = (bf16[256,512]{1,0:T(8,128)(2,1)S(1)}, bf16[256,512]{1,0:T(8,128)(2,1)}, u32[]{:S(2)}) copy-start(bf16[256,512]{1,0:T(8,128)(2,1)} %get-tuple-element.63.refs_4_.refs_7_) | copy-start | bytes 786436
  328.7 73.5 %copy-start.2 = (bf16[256,512]{1,0:T(8,128)(2,1)S(1)}, bf16[256,512]{1,0:T(8,128)(2,1)}, u32[]{:S(2)}) copy-start(bf16[256,512]{1,0:T(8,128)(2,1)} %get-tuple-element.64.refs_5_.refs_8_) | copy-start | bytes 786436
  328.7 73.5 %copy-start.3 = (bf16[256,512]{1,0:T(8,128)(2,1)S(1)}, bf16[256,512]{1,0:T(8,128)(2,1)}, u32[]{:S(2)}) copy-start(bf16[256,512]{1,0:T(8,128)(2,1)} %get-tuple-element.65.refs_6_.refs_9_) | copy-start | bytes 786436
  328.7 73.5 %copy-start.4 = (bf16[256,512]{1,0:T(8,128)(2,1)S(1)}, bf16[256,512]{1,0:T(8,128)(2,1)}, u32[]{:S(2)}) copy-start(bf16[256,512]{1,0:T(8,128)(2,1)} %get-tuple-element.66.refs_7_.refs_10_) | copy-start | bytes 786436
  328.7 73.5 %copy-start.5 = (bf16[256,512]{1,0:T(8,128)(2,1)S(1)}, bf16[256,512]{1,0:T(8,128)(2,1)}, u32[]{:S(2)}) copy-start(bf16[256,512]{1,0:T(8,128)(2,1)} %get-tuple-element.67.refs_8_.refs_11_) | copy-start | bytes 786436
  402.2 1.0 copy-start.6
  403.2 0.9 copy-start.7
  404.2 0.9 copy-start.8
  477.0 1.2 copy-start.9
  643.1 23.7 %slice-start = ((s8[16777216]{0:T(1024)(128)(4,1)}), s8[4194304]{0:T(1024)(128)(4,1)S(1)}, s32[]{:S(2)}) async-start(s8[16777216]{0:T(1024)(128)(4,1)} %bitcast.15), calls=%async_computation | async-start | bytes 8388608
  643.1 23.7 %slice-start.1 = ((s8[16777216]{0:T(1024)(128)(4,1)}), s8[4194304]{0:T(1024)(128)(4,1)S(1)}, s32[]{:S(2)}) async-start(s8[16777216]{0:T(1024)(128)(4,1)} %bitcast.15), calls=%async_computation.1 | async-start | bytes 8388608
  651.6 15.2 %slice-start.2 = ((s8[16777216]{0:T(1024)(128)(4,1)}), s8[4194304]{0:T(1024)(128)(4,1)S(1)}, s32[]{:S(2)}) async-start(s8[16777216]{0:T(1024)(128)(4,1)} %bitcast.15), calls=%async_computation.2 | async-start | bytes 8388608
  651.6 15.2 %slice-start.3 = ((s8[16777216]{0:T(1024)(128)(4,1)}), s8[4194304]{0:T(1024)(128)(4,1)S(1)}, s32[]{:S(2)}) async-start(s8[16777216]{0:T(1024)(128)(4,1)} %bitcast.15), calls=%async_computation.3 | async-start | bytes 8388608

commit v2 on v1

--- a/solution.py
+++ b/solution.py
@@ -5,7 +5,9 @@
 from jax.experimental.pallas import tpu as pltpu
 
 T, D, FF = 2048, 512, 8192
-C = 512
+C = 256
+UNROLL = 4
+CB = 512
 NT = (((1,), (1,)), ((), ()))
 
 def dot(a, b):
@@ -14,12 +16,18 @@
 def dot_nt(a, b):
     return lax.dot_general(a, b, NT, preferred_element_type=jnp.float32)
 
+def by_rows(body):
+    lax.fori_loop(0, T // 256, lambda c, _: (body(pl.ds(pl.multiple_of(c * 256, 256), 256)), 0)[1], 0)
+
 def norm_to(h_ref, a_ref):
-    wide = h_ref[...].astype(jnp.float32)
-    scale = lax.rsqrt(jnp.mean(wide * wide, -1, keepdims=True) + 1e-6)
-    a_ref[...] = (wide * scale).astype(jnp.bfloat16)
-
-def fwd_kernel(x, wg, wu, wd, h1, a_s, acc):
+    def some(rows):
+        wide = h_ref[rows, :].astype(jnp.float32)
+        scale = lax.rsqrt(jnp.mean(wide * wide, -1, keepdims=True) + 1e-6)
+        a_ref[rows, :] = (wide * scale).astype(jnp.bfloat16)
+
+    by_rows(some)
+
+def fwd_kernel(x, wg, wu, wd, h1, gates, ups, a_s, acc):
     k = pl.program_id(0)
 
     @pl.when(k == 0)
@@ -32,33 +40,38 @@
         a = a_s[rows, :]
         gate = dot(a, wg[0])
         up = dot(a, wu[0])
+        gates[rows, :] = gate
+        ups[rows, :] = up
         act = (gate * jax.nn.sigmoid(gate) * up).astype(jnp.bfloat16)
         acc[rows, :] += dot(act, wd[0])
         return 0
 
-    lax.fori_loop(0, T // C, chunk, 0)
+    lax.fori_loop(0, T // C, chunk, 0, unroll=UNROLL)
 
     @pl.when(k == pl.num_programs(0) - 1)
     def _():
         h1[...] = x[...] + acc[...].astype(jnp.bfloat16)
 
-def forward(x, wg, wu, wd, layer, F=512):
+def forward(x, wg, wu, wd, layer, F=1024):
+    one = pl.Buffered(1)
     return pl.pallas_call(
         fwd_kernel,
         grid=(FF // F,),
         in_specs=[
-            pl.BlockSpec((T, D), lambda k: (0, 0)),
+            pl.BlockSpec((T, D), lambda k: (0, 0), pipeline_mode=one),
             pl.BlockSpec((1, D, F), lambda k: (layer, 0, k)),
             pl.BlockSpec((1, D, F), lambda k: (layer, 0, k)),
             pl.BlockSpec((1, F, D), lambda k: (layer, k, 0)),
         ],
-        out_specs=pl.BlockSpec((T, D), lambda k: (0, 0)),
-        out_shape=jax.ShapeDtypeStruct((T, D), jnp.bfloat16),
+        out_specs=[pl.BlockSpec((T, D), lambda k: (0, 0))] + [pl.BlockSpec((T, F), lambda k: (0, k))] * 2,
+        out_shape=[jax.ShapeDtypeStruct((T, D), jnp.bfloat16)] + [jax.ShapeDtypeStruct((T, FF), jnp.float32)] * 2,
         scratch_shapes=[pltpu.VMEM((T, D), jnp.bfloat16), pltpu.VMEM((T, D), jnp.float32)],
         cost_estimate=pl.CostEstimate(flops=6 * T * D * FF, bytes_accessed=3 * D * FF * 2, transcendentals=0),
-        compiler_params=pltpu.CompilerParams(vmem_limit_bytes=56 << 20, dimension_semantics=("arbitrary",)),
+        compiler_params=pltpu.CompilerParams(vmem_limit_bytes=60 << 20, dimension_semantics=("arbitrary",)),
     )(x, wg, wu, wd)
 
+HOSTED = 2
+SCHEDULE = ((0, 0, 0), (1, 0, 1), (1, 1, 0), (2, 1, 1), (4, 2, 0), (5, 2, 1), (6, 3, 0), (7, 3, 1))
 MESH = pl.DeviceIdType.MESH
 ORDERS = ((0, 1, 2), (1, 2, 0), (2, 0, 1))
 
@@ -93,7 +106,7 @@
         self.me, self.at = place()
 
     def rows(self, s):
-        return pl.ds(s * self.R, self.R)
+        return pl.ds(pl.multiple_of(s * self.R, self.R), self.R)
 
     def copy(self, step, p, s):
         own = self.buf[p][0]
@@ -144,16 +157,16 @@
                 for axis in order[: step - 1]:
                     index[axis] = self.at[axis]
                 index[order[step - 1]] = 1 - self.at[order[step - 1]]
-                n = i // max(1, self.R // 64)
+                n = i // (self.R // 64)
                 for axis in free:
                     index[axis] = n % 2
                     n = n // 2
-                small = min(64, self.R)
-                rows = pl.ds(pl.multiple_of(s * self.R + i % (self.R // small) * small, small), small)
+                rows = pl.ds(pl.multiple_of(s * self.R + i % (self.R // 64) * 64, 64), 64)
                 self.buf[p][0][(*index, rows, slice(None))] = self.summed(p, step, index, rows).astype(jnp.bfloat16)
                 return 0
 
-            lax.fori_loop(0, (1 << len(free)) * max(1, self.R // 64), block, 0)
+            trips = (1 << len(free)) * (self.R // 64)
+            lax.fori_loop(0, trips, block, 0, unroll=min(2, trips))
             self.copy(step, p, s).start()
 
     def finish(self, s, outs):
@@ -178,29 +191,32 @@
     da_out = refs.pop(0) if need_da else None
     if hosts:
         summed, refs = refs[:3], refs[3:]
-    a_s, aT, dhT, dg_s, du_s, act_s = refs[:6]
-    refs = refs[6:]
+    a_s, aT, dhT = refs[:3]
+    terms, sums, refs = (refs[3:6], refs[6:9]), refs[9:12], refs[12:]
     acc = refs.pop(0) if need_da else None
     da_sem = refs.pop(0) if need_da and last else None
     k = pl.program_id(0)
     if hosts:
-        scatter = Scatter(g_in, refs, 1)
+        scatter = Scatter(g_in, refs, HOSTED)
 
         @pl.when(k == 0)
         def _():
             greet((8, 4, 2, 1))
-            scatter.start(0)
-
-        for step, when in ((1, 2), (2, 5), (3, 7)):
+
+        for when, step, s in SCHEDULE:
             @pl.when(k == when)
             def _():
-                scatter.advance(step, 0)
+                scatter.advance(step, s) if step else scatter.start(s)
 
     @pl.when(k == 0)
     def _():
         norm_to(h, a_s)
-        aT[...] = a_s[...].T
-        dhT[...] = dh[...].T
+
+        def turn(rows):
+            aT[:, rows] = a_s[rows, :].T
+            dhT[:, rows] = dh[rows, :].T
+
+        by_rows(turn)
         if need_da:
             if last:
                 copy = pltpu.make_async_copy(da_in, acc, da_sem)
@@ -209,32 +225,47 @@
             else:
                 acc[...] = jnp.zeros_like(acc)
 
-    def chunk(c, _):
-        rows = pl.ds(pl.multiple_of(c * C, C), C)
-        a = a_s[rows, :]
-        dy = dh[rows, :]
-        for b in range(2):
-            cols = slice(b * 256, b * 256 + 256)
-            gate = dot(a, wg[b][0])
-            up = dot(a, wu[b][0])
-            dact = dot_nt(dy, wd[b][0]).astype(jnp.bfloat16).astype(jnp.float32)
-            s = jax.nn.sigmoid(gate)
-            silu = gate * s
-            act_s[rows, cols] = (silu * up).astype(jnp.bfloat16)
-            du_s[rows, cols] = (dact * silu).astype(jnp.bfloat16)
-            dg_s[rows, cols] = (dact * up * (s + silu * (1.0 - s))).astype(jnp.bfloat16)
-        if need_da:
-            t = acc[rows, :]
-            for b in range(2):
-                cols = slice(b * 256, b * 256 + 256)
-                t += dot_nt(dg_s[rows, cols], wg[b][0]) + dot_nt(du_s[rows, cols], wu[b][0])
-            acc[rows, :] = t
-        return 0
-
-    lax.fori_loop(0, T // C, chunk, 0)
-    gg[...] = dot(aT[...], dg_s[...]).astype(jnp.bfloat16).reshape(16, 32, 512)
-    gu[...] = dot(aT[...], du_s[...]).astype(jnp.bfloat16).reshape(16, 32, 512)
-    gd[...] = dot(dhT[...], act_s[...]).T.astype(jnp.bfloat16).reshape(2, 256, 512)
+    def states(c, b):
+        rows = slice(c * CB, c * CB + CB)
+        cols = slice(b * 256, b * 256 + 256)
+        dg_s, du_s, act_s = terms[c % 2]
+        gate = dot(a_s[rows, :], wg[b][0]) if need_da else wg[b][rows, :]
+        up = dot(a_s[rows, :], wu[b][0]) if need_da else wu[b][rows, :]
+        dact = dot_nt(dh[rows, :], wd[b][0]).astype(jnp.bfloat16).astype(jnp.float32)
+        s = jax.nn.sigmoid(gate)
+        silu = gate * s
+        act_s[:, cols] = (silu * up).astype(jnp.bfloat16)
+        du_s[:, cols] = (dact * silu).astype(jnp.bfloat16)
+        dg_s[:, cols] = (dact * up * (s + silu * (1.0 - s))).astype(jnp.bfloat16)
+
+    def weights(c, i):
+        left = dhT if i == 2 else aT
+        new = dot(left[:, c * CB : c * CB + CB], terms[c % 2][i][...])
+        if c:
+            new += sums[i][...]
+        if c < T // CB - 1:
+            sums[i][...] = new
+        elif i == 2:
+            gd[...] = new.T.astype(jnp.bfloat16).reshape(2, 256, 512)
+        else:
+            (gg, gu)[i][...] = new.astype(jnp.bfloat16).reshape(16, 32, 512)
+
+    for c in range(T // CB + 1):
+        if c < T // CB:
+            states(c, 0)
+        if c:
+            weights(c - 1, 0)
+        if c < T // CB:
+            states(c, 1)
+        if c:
+            weights(c - 1, 1)
+            weights(c - 1, 2)
+        if need_da and c < T // CB:
+            rows = slice(c * CB, c * CB + CB)
+            dg_s, du_s, _ = terms[c % 2]
+            acc[rows, :] += sum(
+                dot_nt(t[:, b * 256 : b * 256 + 256], w[b][0]) for b in range(2) for t, w in ((dg_s, wg), (du_s, wu))
+            )
 
     if need_da:
         @pl.when(k == pl.num_programs(0) - 1)
@@ -242,16 +273,20 @@
             if not last:
                 da_out[...] = acc[...]
             else:
-                wide = h[...].astype(jnp.float32)
-                scale = lax.rsqrt(jnp.mean(wide * wide, -1, keepdims=True) + 1e-6)
-                da = acc[...].astype(jnp.bfloat16).astype(jnp.float32)
-                along = jnp.mean(da * wide, -1, keepdims=True)
-                da_out[...] = dh[...] + (da * scale - wide * (scale * scale * scale * along)).astype(jnp.bfloat16)
+                def some(rows):
+                    wide = h[rows, :].astype(jnp.float32)
+                    scale = lax.rsqrt(jnp.mean(wide * wide, -1, keepdims=True) + 1e-6)
+                    da = acc[rows, :].astype(jnp.bfloat16).astype(jnp.float32)
+                    along = jnp.mean(da * wide, -1, keepdims=True)
+                    da_out[rows, :] = dh[rows, :] + (da * scale - wide * (scale * scale * scale * along)).astype(jnp.bfloat16)
+
+                by_rows(some)
 
     if hosts:
         @pl.when(k == pl.num_programs(0) - 1)
         def _():
-            scatter.finish(0, summed)
+            for s in range(HOSTED):
+                scatter.finish(s, summed)
 
 G = jax.ShapeDtypeStruct((16, 256, 512), jnp.bfloat16)
 OWN = jax.ShapeDtypeStruct((256, 512), jnp.bfloat16)
@@ -265,9 +300,11 @@
     outs = [G, G, G]
     out_specs = [pl.BlockSpec((16, 32, 512), lambda k: (0, k, 0))] * 2 + [pl.BlockSpec((2, 256, 512), lambda k: (k, 0, 0))]
     scratch = [pltpu.VMEM((T, D), jnp.bfloat16), pltpu.VMEM((D, T), jnp.bfloat16), pltpu.VMEM((D, T), jnp.bfloat16)]
-    scratch += [pltpu.VMEM((T, 512), jnp.bfloat16)] * 3
+    scratch += [pltpu.VMEM((CB, 512), jnp.bfloat16)] * 6 + [pltpu.VMEM((512, 512), jnp.float32)] * 3
     args = [h, dh, wg, wg, wu, wu, wd, wd]
     in_specs = [whole, whole] + wide * 2 + tall
+    if not need_da:
+        in_specs[2:6] = [pl.BlockSpec((T, 256), lambda k, b=b: (0, (2 * k + b) * 2 + half)) for b in range(2)] * 2
     if need_da:
         outs.append(jax.ShapeDtypeStruct((T, D), jnp.bfloat16 if last else jnp.float32))
         out_specs.append(whole)
@@ -282,7 +319,7 @@
         in_specs += [pl.BlockSpec(memory_space=pl.ANY)] * 3
         outs += [OWN] * 3
         out_specs += [pl.BlockSpec((256, 512), lambda k: (0, 0))] * 3
-        scratch += rs_scratch(1)
+        scratch += rs_scratch(HOSTED)
         params = {"collective_id": number, "has_side_effects": True}
     out = pl.pallas_call(
         functools.partial(bwd_kernel, need_da, last, hosts),
@@ -304,16 +341,13 @@
     parts, snd, rcv = refs[RS_REFS:]
     me, _ = place()
     greet(range(1, 16))
-    for t in range(TAIL + 4):
-        for step in range(4, -1, -1):
-            s = t - step
-            if 0 <= s < TAIL:
-                if step == 0:
-                    scatter.start(s)
-                elif step < 4:
-                    scatter.advance(step, s)
-                else:
-                    scatter.finish(s, (a, b, c))
+    def each(act):
+        lax.fori_loop(0, TAIL, lambda s, _: (act(s), 0)[1], 0)
+
+    each(scatter.start)
+    for step in (1, 2, 3):
+        each(lambda s: scatter.advance(step, s))
+    each(lambda s: scatter.finish(s, (a, b, c)))
     square = jnp.zeros((1, 512), jnp.float32)
     for ref in (*done, a, b, c):
         wide = ref[...].astype(jnp.float32)
@@ -457,11 +491,11 @@
     def step(x, dy, *arrays):
         x, dy = x[0], dy[0]
         w, m, v = (arrays[i : i + 3] for i in (0, 3, 6))
-        h1 = forward(x, *w, 0)
+        h1, *gates = forward(x, *w, 0)
         g1a, da, _ = backward(h1, dy, *w, 1, 0, True)
         g1b, dh, s1a = backward(h1, dy, *w, 1, 1, True, da=da, g=g1a, number=1)
-        g0a, _, s1b = backward(x, dh, *w, 0, 0, False, g=g1b, number=2)
-        g0b, _, s0a = backward(x, dh, *w, 0, 1, False, g=g0a, number=3)
+        g0a, _, s1b = backward(x, dh, *gates, w[2], 0, 0, False, g=g1b, number=2)
+        g0b, _, s0a = backward(x, dh, *gates, w[2], 0, 1, False, g=g0a, number=3)
         *s0b, total = tail(g0b, [*s1a, *s1b, *s0a])
         new = update(lax.axis_index("dp"), total, [*s0a, *s0b, *s1a, *s1b], w, m, v)
         return (*gather(new[:3]), *new[3:])

time: 673 us -> 640 us (0.951); the launches traced: 673 us -> 631 us
  Pallas kernels: 638 us -> 596 us
    pallas_call x4, Pallas kernels: 333 us -> 298 us  [backward(): pl.pallas_call(functools.partial(bwd_kernel, need_da, last, hosts), grid=...]
    unnamed x31 -> x33, local copies, waits for them, and re-layouts: 33.9 us -> 33.9 us
where the time goes in v2:
time: 640 us; the launch traced here: 631 us
  Pallas kernels  596 us (93%)
  local copies, waits for them, and re-layouts  33.9 us (5%)
    pallas_call x4, Pallas kernels, backward(): pl.pallas_call(functools.partial(bwd_kernel, need_da, last, hosts), grid=...  298 us
    pallas_call x1, Pallas kernels, gather(): pl.pallas_call(gather_kernel, in_specs=[pl.BlockSpec(memory_space=pltpu.V...  165 us
    pallas_call x1, Pallas kernels, forward(): pl.pallas_call(fwd_kernel, grid=(FF // F,), in_specs=[pl.BlockSpec((T, D)...  67.2 us
    pallas_call x1, Pallas kernels, tail(): pl.pallas_call(tail_kernel, in_specs=[pl.BlockSpec(memory_space=pl.ANY)]...  51.8 us
    unnamed x33, local copies, waits for them, and re-layouts  33.9 us
    pallas_call x1, Pallas kernels, update(): pl.pallas_call(update_kernel, grid_spec=pltpu.PrefetchScalarGridSpec(num_...  14.1 us

profile of v2, /device:TPU:0, one launch (start us, length us, event | category | flops | bytes accessed | tf_op | source)
XLA Modules:
  0.0 631.0 jit_solution(5535560127686781368)
XLA Ops:
  0.6 67.2 %shard_map.178 = (bf16[2048,512]{1,0:T(8,128)(2,1)}, f32[2048,8192]{1,0:T(8,128)}, f32[2048,8192]{1,0:T(8,128)}) custom-call(bf16[2048,512]{1,0:T(8,128)(2,1)} %bitcast.17, bf16[2,512,8192]{2,1,0:T(8,128)(2,1)} %refs_12_.1, bf16[2,512,8192]{2,1,0:T(8,128)(2,1)} %refs_13_.1, bf16[2,8192,512]{2,1,0:T(8,128)(2,1)} %refs_14_.1), custom_call_target="tpu_custom_call" | custom-call | flops 51539607552 | bytes 25165824 | tf_op jit(solution)/shard_map/pallas_call | solution.py:57
  67.8 83.2 %shard_map.179 = (bf16[16,256,512]{2,1,0:T(8,128)(2,1)}, bf16[16,256,512]{2,1,0:T(8,128)(2,1)}, bf16[16,256,512]{2,1,0:T(8,128)(2,1)}, f32[2048,512]{1,0:T(8,128)}) custom-call(bf16[2048,512]{1,0:T(8,128)(2,1)} %get-tuple-element.51.refs_0_, bf16[2048,512]{1,0:T(8,128)(2,1)} %bitcast.29, bf16[2,512,8192]{2,1,0:T(8,128)(2,1)} %refs_12_.1, ...), custom_call_target="tpu_custom_call" | custom-call | flops 68719476736 | bytes 25165824 | tf_op jit(solution)/shard_map/pallas_call | solution.py:324
  151.0 93.8 %shard_map.180 = (bf16[16,256,512]{2,1,0:T(8,128)(2,1)}, bf16[16,256,512]{2,1,0:T(8,128)(2,1)}, bf16[16,256,512]{2,1,0:T(8,128)(2,1)}, bf16[2048,512]{1,0:T(8,12...) custom-call(bf16[2048,512]{1,0:T(8,128)(2,1)} %get-tuple-element.51.refs_0_, ...), custom_call_target="tpu_custom_call" | custom-call | flops 68719476736 | bytes 25165824 | tf_op jit(solution)/shard_map/pallas_call | solution.py:324
  244.8 61.0 %shard_map.181 = (bf16[16,256,512]{2,1,0:T(8,128)(2,1)}, bf16[16,256,512]{2,1,0:T(8,128)(2,1)}, bf16[16,256,512]{2,1,0:T(8,128)(2,1)}, bf16[256,512]{1,0:T(8,128...) custom-call(bf16[2048,512]{1,0:T(8,128)(2,1)} %bitcast.18, bf16[2048,512]{1,0:T(8,128)(2,1)} %get-tuple-element.56.refs_1_, ...), custom_call_target="tpu_custom_call" | custom-call | flops 51539607552 | bytes 25165824 | tf_op jit(solution)/shard_map/pallas_call | solution.py:324
  305.8 0.0 copy-start
  305.8 0.0 copy-start.1
  305.8 0.0 copy-start.2
  305.8 0.0 copy-start.3
  305.8 0.0 copy-start.4
  305.8 0.0 copy-start.5
  305.9 60.0 %shard_map.182 = (bf16[16,256,512]{2,1,0:T(8,128)(2,1)}, bf16[16,256,512]{2,1,0:T(8,128)(2,1)}, bf16[16,256,512]{2,1,0:T(8,128)(2,1)}, bf16[256,512]{1,0:T(8,128...) custom-call(bf16[2048,512]{1,0:T(8,128)(2,1)} %bitcast.19, bf16[2048,512]{1,0:T(8,128)(2,1)} %get-tuple-element.56.refs_1_, ...), custom_call_target="tpu_custom_call" | custom-call | flops 51539607552 | bytes 25165824 | tf_op jit(solution)/shard_map/pallas_call | solution.py:324
  365.9 0.0 copy-done
  365.9 0.0 copy-done.1
  365.9 0.0 copy-done.2
  365.9 0.0 copy-done.3
  365.9 0.0 copy-done.4
  365.9 0.0 copy-done.5
  365.9 0.0 copy-start.6
  365.9 0.9 copy-done.6
  366.9 0.0 copy-start.8
  366.9 0.9 copy-done.8
  367.8 0.0 copy-start.9
  367.8 0.9 copy-done.9
  368.8 0.0 copy-start.7
  368.8 51.8 %shard_map.183 = (bf16[256,512]{1,0:T(8,128)(2,1)S(1)}, bf16[256,512]{1,0:T(8,128)(2,1)S(1)}, bf16[256,512]{1,0:T(8,128)(2,1)S(1)}, f32[8,128]{1,0:T(8,128)S(1)}) custom-call(bf16[2,2,2,2,256,512]{5,4,3,2,1,0:T(8,128)(2,1)} %bitcast.26, bf16[2,2,2,2,256,512]{5,4,3,2,1,0:T(8,128)(2,1)} %bitcast.27, bf16[2,2,2,2,256,512]{5,4,3,2,1,0:T(8,128)(2,1)} %bitcast.28, ...), custom_call_target="tpu_custom_call" | custom-call | tf_op jit(solution)/shard_map/pallas_call | solution.py:371
  420.6 0.0 copy-done.7
  420.6 14.1 %shard_map.184 = (bf16[2,32,8192]{2,1,0:T(8,128)(2,1)S(1)}, bf16[2,32,8192]{2,1,0:T(8,128)(2,1)S(1)}, bf16[2,512,512]{2,1,0:T(8,128)(2,1)}, f32[2,32,8192]{2,1,0...) custom-call(s32[1]{0:T(128)} %bitcast.me, ...), custom_call_target="tpu_custom_call" | custom-call | tf_op jit(solution)/shard_map/pallas_call | solution.py:412
  434.6 0.0 copy-start.10
  434.6 1.2 copy-done.10
  435.9 164.8 %shard_map.185 = (bf16[2,512,8192]{2,1,0:T(8,128)(2,1)S(1)}, bf16[2,512,8192]{2,1,0:T(8,128)(2,1)}, bf16[2,8192,512]{2,1,0:T(8,128)(2,1)}) custom-call(bf16[2,32,8192]{2,1,0:T(8,128)(2,1)S(1)} %get-tuple-element.81.refs_0_, bf16[2,32,8192]{2,1,0:T(8,128)(2,1)S(1)} %get-tuple-element.82.refs_1_, bf16[2,512,512]{2,1,0:T(8,128)(2,1)S(1)} %copy-done.10), custom_call_target="tpu_custom_call" | custom-call | tf_op jit(solution)/shard_map/pallas_call | solution.py:478
  600.7 0.0 slice-start
  600.7 0.0 slice-start.1
  600.7 8.5 %copy.23 = bf16[2,512,8192]{2,1,0:T(8,128)(2,1)} copy(bf16[2,512,8192]{2,1,0:T(8,128)(2,1)S(1)} %get-tuple-element.102) | data formatting | bytes 33554432
  609.2 0.0 slice-start.2
  609.2 0.0 slice-start.3
  609.2 15.2 %copy.24 = bf16[2,512,8192]{2,1,0:T(8,128)(2,1)} copy(bf16[2,512,8192]{2,1,0:T(8,128)(2,1)} %get-tuple-element.103) | data formatting | bytes 33554432
  624.4 0.0 slice-done
  624.4 0.0 slice-done.1
  624.4 0.0 slice-done.2
  624.4 0.0 slice-done.3
  624.4 6.2 copy.25
  (1 shorter events, 0.0 us)
Async XLA Ops:
  305.8 60.1 %copy-start = (bf16[256,512]{1,0:T(8,128)(2,1)S(1)}, bf16[256,512]{1,0:T(8,128)(2,1)}, u32[]{:S(2)}) copy-start(bf16[256,512]{1,0:T(8,128)(2,1)} %get-tuple-element.68.refs_3_.refs_6_) | copy-start | bytes 786436
  305.8 60.1 %copy-start.1 = (bf16[256,512]{1,0:T(8,128)(2,1)S(1)}, bf16[256,512]{1,0:T(8,128)(2,1)}, u32[]{:S(2)}) copy-start(bf16[256,512]{1,0:T(8,128)(2,1)} %get-tuple-element.69.refs_4_.refs_7_) | copy-start | bytes 786436
  305.8 60.1 %copy-start.2 = (bf16[256,512]{1,0:T(8,128)(2,1)S(1)}, bf16[256,512]{1,0:T(8,128)(2,1)}, u32[]{:S(2)}) copy-start(bf16[256,512]{1,0:T(8,128)(2,1)} %get-tuple-element.70.refs_5_.refs_8_) | copy-start | bytes 786436
  305.8 60.1 %copy-start.3 = (bf16[256,512]{1,0:T(8,128)(2,1)S(1)}, bf16[256,512]{1,0:T(8,128)(2,1)}, u32[]{:S(2)}) copy-start(bf16[256,512]{1,0:T(8,128)(2,1)} %get-tuple-element.71.refs_6_.refs_9_) | copy-start | bytes 786436
  305.8 60.1 %copy-start.4 = (bf16[256,512]{1,0:T(8,128)(2,1)S(1)}, bf16[256,512]{1,0:T(8,128)(2,1)}, u32[]{:S(2)}) copy-start(bf16[256,512]{1,0:T(8,128)(2,1)} %get-tuple-element.72.refs_7_.refs_10_) | copy-start | bytes 786436
  305.8 60.1 %copy-start.5 = (bf16[256,512]{1,0:T(8,128)(2,1)S(1)}, bf16[256,512]{1,0:T(8,128)(2,1)}, u32[]{:S(2)}) copy-start(bf16[256,512]{1,0:T(8,128)(2,1)} %get-tuple-element.73.refs_8_.refs_11_) | copy-start | bytes 786436
  365.9 1.0 copy-start.6
  366.9 0.9 copy-start.8
  367.8 0.9 copy-start.9
  368.8 51.8 %copy-start.7 = (bf16[256,512]{1,0:T(8,128)(2,1)S(1)}, bf16[256,512]{1,0:T(8,128)(2,1)}, u32[]{:S(2)}) copy-start(bf16[256,512]{1,0:T(8,128)(2,1)} %get-tuple-element.74.refs_9_.refs_0_) | copy-start | bytes 786436
  434.6 1.2 copy-start.10
  600.7 23.7 %slice-start = ((s8[16777216]{0:T(1024)(128)(4,1)}), s8[4194304]{0:T(1024)(128)(4,1)S(1)}, s32[]{:S(2)}) async-start(s8[16777216]{0:T(1024)(128)(4,1)} %bitcast.15), calls=%async_computation | async-start | bytes 8388608
  600.7 23.7 %slice-start.1 = ((s8[16777216]{0:T(1024)(128)(4,1)}), s8[4194304]{0:T(1024)(128)(4,1)S(1)}, s32[]{:S(2)}) async-start(s8[16777216]{0:T(1024)(128)(4,1)} %bitcast.15), calls=%async_computation.1 | async-start | bytes 8388608
  609.2 15.2 %slice-start.2 = ((s8[16777216]{0:T(1024)(128)(4,1)}), s8[4194304]{0:T(1024)(128)(4,1)S(1)}, s32[]{:S(2)}) async-start(s8[16777216]{0:T(1024)(128)(4,1)} %bitcast.15), calls=%async_computation.2 | async-start | bytes 8388608
  609.2 15.2 %slice-start.3 = ((s8[16777216]{0:T(1024)(128)(4,1)}), s8[4194304]{0:T(1024)(128)(4,1)S(1)}, s32[]{:S(2)}) async-start(s8[16777216]{0:T(1024)(128)(4,1)} %bitcast.15), calls=%async_computation.3 | async-start | bytes 8388608
